TPU v7x, 256 devices: a whole 4x4x8 slice. The times are simulated.
256 devices in a mesh: freq: 8 (over x, core), rec: 32 (over z, y).
Axes of the slice: x: 4, y: 4, z: 8, core: 2. Of those that a mesh axis runs over, the one named last changes fastest.
Arguments:
- response_real: float32 [96, 1536, 1536], P('freq', 'rec'), may hold values from -0.109375 to 0.109375
- response_imaginary: float32 [96, 1536, 1536], P('freq', 'rec'), may hold values from -0.109375 to 0.109375
- focus: float32 [1536, 96, 128], P('rec', 'freq'), may hold values from -6 to 6
- initial: float32 [1536, 96, 128], P('rec', 'freq'), may hold values from -6 to 6
- onset: int32 [1536, 64], P('rec'), may hold values from 24 to 167
Outputs:
- focus_next: float32 [1536, 96, 128], P('rec', 'freq')
All inputs are finite; a program needn't handle non-finite values.
Results may differ from a plain program's by a relative error of at most 0.0003.
Values sent between devices are 32-bit elements; how exact they have to be, the bound alone decides.
A program may use at most 128 MiB of HBM per device.

v0:
```python
import math

import jax
import jax.numpy as jnp
from jax import lax
from jax.sharding import Mesh
from jax.sharding import PartitionSpec as P

REC = ("rec_0", "rec_1")


def sum_by_axis(total, axes):
    for axis in axes:
        total = lax.psum_scatter(total, axis, scatter_dimension=0, tiled=True)
    return total


def tables(freqs):
    samples = 2 * freqs
    order = lax.iota(jnp.int32, freqs)
    sample = lax.iota(jnp.int32, samples)
    phase = order[:, None] * sample[None, :] % samples
    phases = 2.0 * math.pi / samples * phase.astype(jnp.float32)
    cosine = jnp.cos(phases)
    sine = jnp.sin(phases)
    factor = jnp.where(order == 0, 1.0, 2.0).astype(jnp.float32)[:, None] / samples
    inverse = jnp.stack([factor * cosine, -factor * sine])
    forward = jnp.stack([cosine, -sine])
    return (inverse, forward, sample)


def window(spectrum, onset):
    count, freqs, width = spectrum.shape
    half = width // 2
    inverse, forward, sample = tables(freqs)
    split = spectrum.reshape(count, freqs, 2, half)
    traces = jnp.einsum("nkcp,ckt->ntp", split, inverse, precision=lax.Precision.HIGHEST)
    keep = sample[None, :, None] < onset[:, None, :]
    clipped = jnp.where(keep, traces, 0.0)
    back = jnp.einsum("ntp,ckt->nkcp", clipped, forward, precision=lax.Precision.HIGHEST)
    return back.reshape(count, freqs, width)


def adjoint_terms(real_part, imag_part, values):
    half = values.shape[2] // 2
    first = jnp.einsum("frs,rfq->sfq", real_part, values, precision=lax.Precision.HIGHEST)
    second = jnp.einsum("frs,rfq->sfq", imag_part, values, precision=lax.Precision.HIGHEST)
    return jnp.concatenate(
        [first[..., :half] + second[..., half:], first[..., half:] - second[..., :half]], axis=2
    )


def forward_terms(real_part, imag_part, values):
    half = values.shape[2] // 2
    first = jnp.einsum("frs,sfq->rfq", real_part, values, precision=lax.Precision.HIGHEST)
    second = jnp.einsum("frs,sfq->rfq", imag_part, values, precision=lax.Precision.HIGHEST)
    return jnp.concatenate(
        [first[..., :half] - second[..., half:], first[..., half:] + second[..., :half]], axis=2
    )


def onset_rows(onset):
    owned = onset.shape[0] // lax.axis_size("freq")
    return lax.dynamic_slice_in_dim(onset, lax.axis_index("freq") * owned, owned, 0)


def iterate(response_real, response_imaginary, values, onset):
    local_onset = onset_rows(onset)
    real_cols = response_real
    imag_cols = response_imaginary
    partial_sum = sum_by_axis(adjoint_terms(real_cols, imag_cols, values), REC)
    turned = lax.all_to_all(partial_sum, "freq", split_axis=0, concat_axis=1, tiled=True)
    windowed = window(turned, local_onset)
    returned = lax.all_to_all(windowed, "freq", split_axis=1, concat_axis=0, tiled=True)
    real_cols = response_real
    imag_cols = response_imaginary
    forward = forward_terms(real_cols, imag_cols, lax.all_gather(returned, REC, axis=0, tiled=True))
    receiver_side = lax.all_to_all(forward, "freq", split_axis=0, concat_axis=1, tiled=True)
    clipped = window(receiver_side, local_onset)
    return lax.all_to_all(clipped, "freq", split_axis=1, concat_axis=0, tiled=True)


def on_device(response_real, response_imaginary, focus, initial, onset):
    real_used, imag_used = (response_real, response_imaginary)
    update = iterate(real_used, imag_used, focus, onset)
    return initial - update


def solution(mesh):
    finer = Mesh(mesh.devices.reshape(mesh.shape["freq"], 8, 4), ("freq", "rec_0", "rec_1"))
    in_specs = (
        P("freq", REC, None),
        P("freq", REC, None),
        P(REC, "freq", None),
        P(REC, "freq", None),
        P(REC, None),
    )
    out_specs = P(REC, "freq", None)
    return jax.shard_map(
        on_device, mesh=finer, in_specs=in_specs, out_specs=out_specs, check_vma=False
    )
```

profile of v0, /device:TPU:1, one launch (start us, length us, event | category | flops | bytes accessed | tf_op | source)
XLA Modules:
  0.0 388.9 jit_solution(16803704345804091583)
XLA Ops:
  6.5 2.0 copy-done
  8.5 8.9 %convolution_bitcast_fusion = f32[1536,12,128]{0,2,1:T(8,128)S(1)} fusion(f32[48,12,128]{2,0,1:T(8,128)} %param.7, f32[12,48,1536]{2,1,0:T(8,128)S(1)} %copy-done), kind=kOutput, calls=%fused_computation.1 | convolution fusion | flops 1358954496 | bytes 13271040 | tf_op jit(solution)/shard_map/frs,rfq->sfq/dot_general | solution.py:47
  17.5 8.0 %convolution_bitcast_fusion.1 = f32[1536,12,128]{0,2,1:T(8,128)S(1)} fusion(f32[48,12,128]{2,0,1:T(8,128)S(1)} %copy-done.4, f32[12,48,1536]{2,1,0:T(8,128)S(1)} %copy-done.2), kind=kOutput, calls=%fused_computation.2 | convolution fusion | flops 1358954496 | bytes 13271040 | tf_op jit(solution)/shard_map/frs,rfq->sfq/dot_general | solution.py:46
  25.5 3.5 slice_add_fusion
  29.0 7.3 %pad_maximum_fusion = f32[1536,12,128]{0,2,1:T(8,128)} fusion(f32[1536,12,64]{0,2,1:T(8,128)} %get-tuple-element.6, f32[1536,12,64]{0,2,1:T(8,128)S(1)} %get-tuple-element.5), kind=kLoop, calls=%fused_computation | loop fusion | flops 2359296 | bytes 18874368 | tf_op jit(solution)/shard_map/concatenate | solution.py:48
  36.3 9.6 %copy.44 = f32[1536,1536]{1,0:T(8,128)} copy(f32[1536,1536]{0,1:T(8,128)} %bitcast.81) | data formatting | bytes 18874368
  46.0 108.7 %reduce-scatter.7.cloned.1.call-done = f32[192,1536]{1,0:T(8,128)} async-done(((f32[1536,1536]{1,0:T(8,128)}), f32[192,1536]{1,0:T(8,128)}) %reduce-scatter.7.cloned.1.call-update) | async-done | bytes 1179664
  154.6 2.9 copy.45
  157.5 3.4 copy.15
  161.6 1.1 fusion.11
  162.8 24.4 %reduce-scatter.5.cloned.1.call-done = f32[48,12,128]{2,1,0:T(8,128)} async-done(((f32[192,12,128]{2,1,0:T(8,128)}), f32[48,12,128]{2,1,0:T(8,128)}) %reduce-scatter.5.cloned.1.call-update) | async-done | bytes 294928 | tf_op jit(solution)/shard_map/reduce_scatter | solution.py:14
  187.2 5.7 %all-to-all-start = ((f32[48,12,128]{2,1,0:T(8,128)}), f32[48,12,128]{2,1,0:T(8,128)}, u32[]{:S(2)}, u32[]{:S(2)}) async-start(f32[48,12,128]{2,1,0:T(8,128)} %reduce-scatter.5.cloned.1.call-done), calls=%async_computation.1 | async-start | bytes 786432 | tf_op jit(solution)/shard_map/all_to_all | solution.py:72
  192.9 1.1 fusion.12
  194.0 6.7 %all-to-all-done = f32[48,12,128]{2,1,0:T(8,128)} async-done(((f32[48,12,128]{2,1,0:T(8,128)}), f32[48,12,128]{2,1,0:T(8,128)}, u32[]{:S(2)}, u32[]{:S(2)}) %all-to-all-start) | async-done | bytes 294944 | tf_op jit(solution)/shard_map/all_to_all | solution.py:72
  200.7 1.8 copy.17
  202.5 2.2 reshape.140
  204.6 2.3 fusion.1
  206.9 1.4 convolution_bitcast_fusion.4
  209.2 1.9 copy.20
  211.1 12.6 %all_to_all.66 = f32[6,96,128]{2,0,1:T(8,128)S(1)} all-to-all(f32[6,96,128]{2,0,1:T(8,128)} %copy.20), channel_id=1, replica_groups=mesh['freq'=8,'rec_0'=8,'rec_1'=4] {'freq'}, dimensions={1} | all-to-all | bytes 589824 | tf_op jit(solution)/shard_map/all_to_all | solution.py:74
  224.5 1.7 all_to_all.54
  226.3 100.8 %all-gather.2.cloned.1.call-done = f32[1536,12,128]{2,0,1:T(8,128)} async-done(((f32[48,12,128]{2,0,1:T(8,128)}), f32[1536,12,128]{2,0,1:T(8,128)}) %all-gather.2.cloned.1.call-update) | async-done | bytes 9437200 | tf_op jit(solution)/shard_map/all_gather | solution.py:77
  327.1 9.3 %convolution_bitcast_fusion.6 = f32[48,12,128]{2,0,1:T(8,128)S(1)} fusion(f32[1536,12,128]{2,0,1:T(8,128)} %all-gather.2.cloned.1.call-done, f32[12,48,1536]{2,1,0:T(8,128)S(1)} %copy-done), kind=kOutput, calls=%fused_computation.9 | convolution fusion | flops 1358954496 | bytes 13271040 | tf_op jit(solution)/shard_map/frs,sfq->rfq/dot_general | solution.py:56
  336.4 6.0 %convolution_bitcast_fusion.7 = f32[48,12,128]{2,0,1:T(8,128)S(1)} fusion(f32[1536,12,128]{2,0,1:T(8,128)S(1)} %copy-done.1, f32[12,48,1536]{2,1,0:T(8,128)S(1)} %copy-done.3), kind=kOutput, calls=%fused_computation.10 | convolution fusion | flops 1358954496 | bytes 13271040 | tf_op jit(solution)/shard_map/frs,sfq->rfq/dot_general | solution.py:55
  342.9 13.5 %all_to_all.67 = f32[48,12,128]{2,1,0:T(8,128)S(1)} all-to-all(f32[48,12,128]{2,1,0:T(8,128)S(1)} %copy.23), channel_id=1, replica_groups=mesh['freq'=8,'rec_0'=8,'rec_1'=4] {'freq'}, dimensions={0} | all-to-all | bytes 589824 | tf_op jit(solution)/shard_map/all_to_all | solution.py:78
  357.2 2.2 reshape.142
  359.3 2.3 fusion.3
  361.6 1.4 convolution_bitcast_fusion.2
  363.9 1.9 copy.28
  365.8 12.3 %all_to_all.68 = f32[6,96,128]{2,0,1:T(8,128)S(1)} all-to-all(f32[6,96,128]{2,0,1:T(8,128)} %copy.28), channel_id=1, replica_groups=mesh['freq'=8,'rec_0'=8,'rec_1'=4] {'freq'}, dimensions={1} | all-to-all | bytes 589824 | tf_op jit(solution)/shard_map/all_to_all | solution.py:80
  378.9 1.7 all_to_all.61
  380.6 1.8 sub.11
  (26 shorter events, 5.2 us)
Async XLA Ops:
  6.5 2.0 copy-start
  6.5 148.1 %reduce-scatter.7.cloned.1.call-start = ((), (), s32[]{:S(2)}) async-start(), calls=%async_computation.8 | async-start | bytes 10616832
  8.5 8.9 %copy-start.2 = (f32[12,48,1536]{2,1,0:T(8,128)S(1)}, f32[12,48,1536]{2,1,0:T(8,128)}, u32[]{:S(2)}) copy-start(f32[12,48,1536]{2,1,0:T(8,128)} %param.5) | copy-start | bytes 10616836
  8.5 9.0 %copy-start.4 = (f32[48,12,128]{2,0,1:T(8,128)S(1)}, f32[48,12,128]{2,0,1:T(8,128)}, u32[]{:S(2)}) copy-start(f32[48,12,128]{2,0,1:T(8,128)} %param.7) | copy-start | bytes 884740
  45.9 141.2 %reduce-scatter.5.cloned.1.call-start = ((), (), s32[]{:S(2)}) async-start(), calls=%async_computation.6 | async-start | bytes 1966080 | tf_op jit(solution)/shard_map/reduce_scatter | solution.py:14
  187.2 13.5 %all-to-all-start = ((f32[48,12,128]{2,1,0:T(8,128)}), f32[48,12,128]{2,1,0:T(8,128)}, u32[]{:S(2)}, u32[]{:S(2)}) async-start(f32[48,12,128]{2,1,0:T(8,128)} %reduce-scatter.5.cloned.1.call-done), calls=%async_computation.1 | async-start | bytes 786432 | tf_op jit(solution)/shard_map/all_to_all | solution.py:72
  192.9 134.2 %all-gather.2.cloned.1.call-start = ((), (), s32[]{:S(2)}) async-start(), calls=%async_computation.7 | async-start | bytes 9732096 | tf_op jit(solution)/shard_map/all_gather | solution.py:77
  327.1 9.3 %copy-start.1 = (f32[1536,12,128]{2,0,1:T(8,128)S(1)}, f32[1536,12,128]{2,0,1:T(8,128)}, u32[]{:S(2)}) copy-start(f32[1536,12,128]{2,0,1:T(8,128)} %all-gather.2.cloned.1.call-done) | copy-start | bytes 28311556
  327.1 9.3 %copy-start.3 = (f32[12,48,1536]{2,1,0:T(8,128)S(1)}, f32[12,48,1536]{2,1,0:T(8,128)}, u32[]{:S(2)}) copy-start(f32[12,48,1536]{2,1,0:T(8,128)} %param.5) | copy-start | bytes 10616836
Sparse Core Ops, SparseCore 0:
  46.0 108.5 reduce-scatter.6
  161.0 26.0 reduce-scatter.4
  226.4 100.6 all-gather.1
where the time goes:
time: 390 us; the launch traced here: 389 us
  waiting for transfers between devices  241 us (62%)
  matrix products  39.7 us (10%)
  blocking collectives  38.4 us (10%)
  local copies, waits for them, and re-layouts  36 us (9%)
  other arithmetic  15.2 us (4%)
  between operations  13.2 us (3%)
  starting transfers between devices  5.78 us (1%)
    unnamed x4, waiting for transfers between devices  109 us
    all_gather x1, waiting for transfers between devices, iterate(): lax.all_gather(returned, REC, axis=0, tiled=True)  101 us
    reduce_scatter x1, waiting for transfers between devices, sum_by_axis(): total = lax.psum_scatter(total, axis, scatter_dimension=0, tiled=True)  24.4 us
    unnamed x12, local copies, waits for them, and re-layouts  14.5 us
    all_to_all x1, blocking collectives, iterate(): lax.all_to_all(forward, 'freq', split_axis=0, concat_axis=1, tiled=True)  13.5 us
    all_to_all x1, blocking collectives, iterate(): lax.all_to_all(windowed, 'freq', split_axis=1, concat_axis=0, tiled=True)  12.6 us
    all_to_all x1, blocking collectives, iterate(): lax.all_to_all(clipped, 'freq', split_axis=1, concat_axis=0, tiled=True)  12.3 us
    dot_general x1, matrix products, forward_terms(): jnp.einsum('frs,sfq->rfq', imag_part, values, precision=lax.Precision.HIG...  9.26 us
  transfers between devices with their start and end apart: 4, of which 4 were waited for; matrix products, arithmetic and copies ran while one was open for 1% of the time, Pallas kernels for 0%

commit v1 on v0

v1 whole, which is shorter than its diff:
```python
import functools
import heapq

import jax
import jax.numpy as jnp
import numpy as np
from jax import lax
from jax.experimental import pallas as pl
from jax.experimental.pallas import tpu as pltpu
from jax.sharding import PartitionSpec as P

MESH = pl.DeviceIdType.MESH
BF = jnp.bfloat16
F32 = jnp.float32

NF = 8
NZ, NY = 8, 4
FL = 12
ROWS = 48
SPLIT = 5
CHUNKS = ((0, 24), (24, 24))
RATE = 46.6e3
LATENCY = 1.8


def split(value):
    high = value.astype(BF)
    low = (value - high.astype(F32)).astype(BF)
    return high, low


def dft_tables(freqs):
    samples = 2 * freqs
    phase = np.arange(freqs)[:, None] * np.arange(samples)[None, :] % samples
    angle = 2.0 * np.pi / samples * phase
    cosine, sine = np.cos(angle), np.sin(angle)
    factor = np.where(np.arange(freqs) == 0, 1.0, 2.0)[:, None] / samples
    inverse = np.concatenate([factor * cosine, -factor * sine]).T
    forward = np.concatenate([cosine, -sine])
    out = []
    for table in (inverse, forward):
        table = table.astype(np.float32)
        high = table.astype(jnp.bfloat16)
        low = (table - high.astype(np.float32)).astype(jnp.bfloat16)
        out.append(np.concatenate([high, high, low], axis=1))
    return out


PARTS = {"a": (0, SPLIT), "b": (SPLIT, FL - SPLIT)}


def halves(part, sign):
    start, count = PARTS[part]
    first = (count + 1) // 2 if part == "a" else count // 2
    return (start, first) if sign > 0 else (start + first, count - first)


class Plan:
    def __init__(self):
        self.tasks = {}

    def add(self, name, deps, run, link=None, size=0, dur=0.1, rank=(0,)):
        self.tasks[name] = (tuple(deps), run, link, size, dur, rank)

    def order(self):
        free, arrived, done = {}, {}, {}
        left = dict(self.tasks)
        now, order = 0.0, []
        while left:
            ready, soonest = [], None
            for name, (deps, run, link, size, dur, rank) in left.items():
                when = 0.0
                for dep in deps:
                    when = max(when, arrived.get(dep, 1e9))
                if when <= now:
                    ready.append((rank, name))
                soonest = when if soonest is None else min(soonest, when)
            if not ready:
                if soonest >= 1e9:
                    raise ValueError("cycle")
                now = soonest
                continue
            _, name = min(ready)
            deps, run, link, size, dur, rank = left.pop(name)
            now += dur
            order.append(name)
            if link is None:
                arrived[name] = now
            else:
                start = max(now, free.get(link, 0.0))
                free[link] = start + size / RATE
                arrived[name] = free[link] + LATENCY
            done[name] = now
        self.finish = now
        self.times = arrived
        return order


def kernel(rr, ri, focus, onset, inv, fwd, out, *scratch):
    (part, stage_a1, stage_a2, stage_b1, stage_b2, gathered, xs, x1, y1, x2, y2, made, back,
     send_sem, recv_sem, win_send, win_recv, ret_send, ret_recv) = scratch
    me_f, me_r = lax.axis_index("freq"), lax.axis_index("rec")
    z, y = lax.div(me_r, NY), lax.rem(me_r, NY)

    def at_z(d):
        return lax.rem(z + (d + NZ), NZ) if d else z

    def at_y(d):
        return lax.rem(y + (d + NY), NY) if d else y

    def rec_of(dz, dy):
        return at_z(dz) * NY + at_y(dy)

    barrier = pltpu.get_barrier_semaphore()
    for dz, dy in ((1, 0), (-1, 0), (0, 1), (0, -1)):
        pl.semaphore_signal(barrier, inc=1, device_id=(me_f, rec_of(dz, dy)), device_id_type=MESH)
    for d in range(1, NF):
        pl.semaphore_signal(barrier, inc=1, device_id=(lax.rem(me_f + d, NF), me_r), device_id_type=MESH)
    pl.semaphore_wait(barrier, 4 + NF - 1)

    lane = lax.broadcasted_iota(jnp.int32, (ROWS, 128), 1)
    low_half = lane < 64
    plan = Plan()
    copies, waits = {}, []

    def piece(name, src, dst, target):
        index = len(copies)
        copies[name] = pltpu.make_async_remote_copy(
            src_ref=src, dst_ref=dst, send_sem=send_sem.at[index], recv_sem=recv_sem.at[index],
            device_id=(me_f, target), device_id_type=MESH)
        return copies[name]

    for f in range(FL):
        value = focus[:, f, :]
        turned = pltpu.roll(value, 64, 1)
        xs[f, 0:ROWS, :] = value
        xs[f, ROWS : 2 * ROWS, :] = jnp.where(low_half, turned, -turned)

    def adjoint(start, count):
        def run():
            def step(f, _):
                x_high, x_low = split(xs[f])
                both = jnp.concatenate([x_high, x_low], axis=1)
                for c in range(4):
                    cols = pl.ds(384 * c, 384)
                    high, low = split(jnp.concatenate([rr[f, :, cols], ri[f, :, cols]], axis=0))
                    dims = (((0,), (0,)), ((), ()))
                    one = lax.dot_general(high, both, dims, preferred_element_type=F32)
                    two = lax.dot_general(low, x_high, dims, preferred_element_type=F32)
                    total = one[:, :128] + one[:, 128:] + two
                    part[f, 2 * c : 2 * c + 2] = total.reshape(2, NY, ROWS, 128)
                return _

            lax.fori_loop(start, start + count, step, 0)

        return run

    for name, (start, count) in PARTS.items():
        plan.add("adj" + name, (), adjoint(start, count), dur=8.0 * count / FL, rank=(0, name != "b"))

    slot = {"a1": 0, "a2": 0, "b1": 0, "b2": 0}
    stages = {"a1": stage_a1, "a2": stage_a2, "b1": stage_b1, "b2": stage_b2}

    def staging(kind, count, nr):
        index = slot[kind]
        slot[kind] += 1
        return stages[kind].at[index, pl.ds(0, count), pl.ds(0, nr), :]

    def reduce_piece(name, kind, freqs, dz, dy, rows, target, adds, deps, link, rank):
        start, count = freqs
        r0, nr = rows
        src = part.at[pl.ds(start, count), at_z(dz), at_y(dy), pl.ds(r0, nr), :]
        dst = staging(kind, count, nr)
        copy = piece(name, src, dst, target)
        copies[name] = (copy, dst, start, count)

        def run():
            take(adds, dz, dy, rows)
            copy.start()

        plan.add(name, tuple(adds) + tuple(deps), run, link, count * nr * 512, 0.12, rank)

    def take(adds, dz, dy, rows):
        r0, nr = rows
        for other in adds:
            copy, dst, start, count = copies[other]
            copy.wait_recv()
            where = (pl.ds(start, count), at_z(dz), at_y(dy), pl.ds(r0, nr), slice(None))
            part[where] += dst[...]

    for h, rows in enumerate(CHUNKS):
        deep = NZ // 2
        order_y = (2, 1, -1, 0)
        order_z = (4, 3, -3, 2, -2, 1, -1, 0)
        both_y = {1: (2, 0), -1: (1, -1)}
        both_z = {1: (4, 2, -2, 0), -1: (3, -3, 1, -1)}
        for k in range(deep, 0, -1):
            for place, dy in enumerate(order_y):
                for sign in (1, -1):
                    if k == deep and dy not in both_y[sign]:
                        continue
                    adds = [f"a1{h},{sign},{k + 1},{dy}"] if (k < deep - 1 or (k == deep - 1 and dy in both_y[sign])) else []
                    reduce_piece(f"a1{h},{sign},{k},{dy}", "a1", PARTS["a"], sign * k, dy, rows, rec_of(sign, 0), adds,
                                 ("adja",), ("z", sign), (1, h, 0, -k, place))
        for k in (2, 1):
            for place, dz in enumerate(order_z):
                for sign in (1, -1):
                    if k == 2 and dz not in both_z[sign]:
                        continue
                    adds = [f"b1{h},{sign},2,{dz}"] if k == 1 and dz in both_z[sign] else []
                    reduce_piece(f"b1{h},{sign},{k},{dz}", "b1", PARTS["b"], dz, sign * k, rows, rec_of(0, sign), adds,
                                 ("adjb",), ("y", sign), (1, h, 0, -k, place))

        def first_sum(name, kind, d):
            keys = [f"{kind}{h},{sign},1,{d}" for sign in (1, -1)]

            def run(keys=keys, d=d, rows=rows, kind=kind):
                dz, dy = (0, d) if kind == "a1" else (d, 0)
                take(keys, dz, dy, rows)

            plan.add(name, keys, run, dur=0.12, rank=(0, h, 0))

        for dy in order_y:
            first_sum(f"as{h},{dy}", "a1", dy)
        for dz in order_z:
            first_sum(f"bs{h},{dz}", "b1", dz)
        for sign in (1, -1):
            reduce_piece(f"a2{h},{sign},2", "a2", halves("a", sign), 0, 2 * sign, rows, rec_of(0, sign), [],
                         (f"as{h},2",), ("y", sign), (0, h, 1, -2))
            reduce_piece(f"a2{h},{sign},1", "a2", PARTS["a"], 0, sign, rows, rec_of(0, sign), [f"a2{h},{sign},2"],
                         (f"as{h},{sign}",), ("y", sign), (0, h, 1, -1))
            for k in range(deep, 0, -1):
                freqs = halves("b", sign) if k == deep else PARTS["b"]
                adds = [] if k == deep else [f"b2{h},{sign},{k + 1}"]
                source = 4 if k == deep else sign * k
                reduce_piece(f"b2{h},{sign},{k}", "b2", freqs, sign * k, 0, rows, rec_of(sign, 0), adds,
                             (f"bs{h},{source}",), ("z", sign), (0, h, 1, -k))

        own_keys = [f"a2{h},{sign},1" for sign in (1, -1)] + [f"b2{h},{sign},1" for sign in (1, -1)]

        def own_sum(keys=tuple(own_keys), rows=rows):
            take(keys, 0, 0, rows)

        plan.add(f"own{h}", own_keys + [f"as{h},0", f"bs{h},0"], own_sum, dur=0.2, rank=(0, h, 0))

    def block_of(buffer, freqs, j):
        return buffer.at[freqs, z, y, pl.ds(8 * j, 8), :]

    def out_copy(source, landing, which, j):
        return pltpu.make_async_remote_copy(
            src_ref=source(j), dst_ref=landing.at[pl.ds(FL * me_f, FL)],
            send_sem=win_send.at[which, j], recv_sem=win_recv.at[which, me_f],
            device_id=(j, me_r), device_id_type=MESH)

    def in_wait(landing, which, sender):
        pltpu.make_async_remote_copy(
            src_ref=landing.at[pl.ds(FL * sender, FL)], dst_ref=landing.at[pl.ds(FL * sender, FL)],
            send_sem=win_send.at[which, 0], recv_sem=win_recv.at[which, sender],
            device_id=(sender, me_r), device_id_type=MESH).wait_recv()

    def return_copy(clipped, target, which, d):
        return pltpu.make_async_remote_copy(
            src_ref=clipped.at[pl.ds(FL * d, FL)], dst_ref=target(me_f),
            send_sem=ret_send.at[which, d], recv_sem=ret_recv.at[which, me_f],
            device_id=(d, me_r), device_id_type=MESH)

    def return_wait(target, which, j):
        pltpu.make_async_remote_copy(
            src_ref=target(j), dst_ref=target(j), send_sem=ret_send.at[which, 0],
            recv_sem=ret_recv.at[which, j], device_id=(j, me_r), device_id_type=MESH).wait_recv()

    def window(landing, clipped):
        half = lax.broadcasted_iota(jnp.int32, (NF * FL, 128), 1) < 64
        tops, bottoms = [], []
        for m in range(4):
            first, second = landing[:, 2 * m, :], landing[:, 2 * m + 1, :]
            tops.append(jnp.where(half, first, pltpu.roll(second, 64, 1)))
            bottoms.append(jnp.where(half, pltpu.roll(first, 64, 1), second))
        spectrum = jnp.concatenate([jnp.concatenate(tops, axis=1), jnp.concatenate(bottoms, axis=1)], axis=0)
        high, low = split(spectrum)
        traces = jnp.dot(inv[...], jnp.concatenate([high, low, high], axis=0), preferred_element_type=F32)
        limit = onset[jnp.minimum(me_f, ROWS // 8 - 1)]
        limits = jnp.concatenate([limit[m : m + 1, :] for m in range(4)], axis=1)
        sample = lax.broadcasted_iota(jnp.int32, traces.shape, 0)
        kept = jnp.where(sample < limits, traces, 0.0)
        high, low = split(kept)
        again = jnp.dot(fwd[...], jnp.concatenate([high, low, high], axis=0), preferred_element_type=F32)
        for m in range(4):
            real = again[: NF * FL, 128 * m : 128 * m + 128]
            imag = again[NF * FL :, 128 * m : 128 * m + 128]
            clipped[:, 2 * m, :] = jnp.where(half, real, pltpu.roll(imag, 64, 1))
            clipped[:, 2 * m + 1, :] = jnp.where(half, pltpu.roll(real, 64, 1), imag)

    def window_tasks(which, tag, members, source, landing, clipped, target, deps, rank):
        def scatter():
            for j in members:
                @pl.when(me_f != j)
                def _():
                    out_copy(source, landing, which, j).start()

                @pl.when(me_f == j)
                def _():
                    landing[FL * j : FL * j + FL] = source(j)[...]

        def apply():
            @pl.when((me_f >= members[0]) & (me_f <= members[-1]))
            def _():
                for sender in range(NF):
                    @pl.when(me_f != sender)
                    def _():
                        in_wait(landing, which, sender)

                window(landing, clipped)
                for d in range(NF):
                    @pl.when(me_f != d)
                    def _():
                        return_copy(clipped, target, which, d).start()

                target(me_f)[...] = clipped[pl.ds(FL * me_f, FL)]

        def collect():
            for j in members:
                @pl.when(me_f != j)
                def _():
                    return_wait(target, which, j)

        def drain():
            for j in members:
                @pl.when(me_f != j)
                def _():
                    out_copy(source, landing, which, j).wait_send()

            @pl.when((me_f >= members[0]) & (me_f <= members[-1]))
            def _():
                for d in range(NF):
                    @pl.when(me_f != d)
                    def _():
                        return_copy(clipped, target, which, d).wait_send()

        waits.append(drain)
        size = len(members) * 8 * FL * 512
        plan.add(tag + "out", deps, scatter, ("x", 0), size, 0.3, rank)
        plan.add(tag + "win", (tag + "out",), apply, ("x", 1), size, 1.5, rank)
        plan.add(tag + "in", (tag + "win",), collect, dur=0.2, rank=rank)

    everything = pl.ds(0, FL)
    for h, (r0, nr) in enumerate(CHUNKS):
        members = tuple(range(r0 // 8, (r0 + nr) // 8))
        window_tasks(0, f"w{h}", members, functools.partial(block_of, part, everything), x1, y1,
                     functools.partial(block_of, gathered, everything), (f"own{h}",), (0, h, 0))

    def gather_piece(name, freqs, dz, dy, rows, target, deps, link, rank):
        start, count = freqs
        r0, nr = rows
        where = gathered.at[pl.ds(start, count), at_z(dz), at_y(dy), pl.ds(r0, nr), :]
        copy = piece(name, where, where, target)
        arrivals = [dep for dep in deps if dep in copies]

        def run():
            for dep in arrivals:
                receive(dep)
            copy.start()

        plan.add(name, deps, run, link, count * nr * 512, 0.08, rank)

    received = set()

    def receive(name):
        if name not in received:
            received.add(name)
            copies[name].wait_recv()

    ends = {"a": [], "b": []}
    for h, rows in enumerate(CHUNKS):
        own = f"w{h}in"
        deep = NZ // 2
        for sign in (1, -1):
            gather_piece(f"ya{h},{sign},0", PARTS["a"], 0, 0, rows, rec_of(0, sign), (own,), ("y", sign), (2, h, 0))
            gather_piece(f"zb{h},{sign},0", PARTS["b"], 0, 0, rows, rec_of(sign, 0), (own,), ("z", sign), (2, h, 0))
        for sign in (1, -1):
            gather_piece(f"ya{h},{sign},1", halves("a", sign), 0, -sign, rows, rec_of(0, sign), (f"ya{h},{sign},0",),
                         ("y", sign), (2, h, 0))
            for k in range(1, deep):
                freqs = halves("b", sign) if k == deep - 1 else PARTS["b"]
                gather_piece(f"zb{h},{sign},{k}", freqs, -sign * k, 0, rows, rec_of(sign, 0), (f"zb{h},{sign},{k - 1}",),
                             ("z", sign), (2, h, 0))
        for dy in (0, -1, 1, 2):
            if dy == 0:
                deps = (own,)
            elif dy == 2:
                deps = (f"ya{h},1,1", f"ya{h},-1,1")
            else:
                deps = (f"ya{h},{-dy},0",)
            for sign in (1, -1):
                for k in range(deep):
                    if k == deep - 1 and dy not in both_y[sign]:
                        continue
                    gather_piece(f"za{h},{sign},{k},{dy}", PARTS["a"], -sign * k, dy, rows, rec_of(sign, 0),
                                 deps if k == 0 else (f"za{h},{sign},{k - 1},{dy}",), ("z", sign), (2, h, 1, k))
                    ends["a"].append(f"za{h},{sign},{k},{dy}")
        for dz in (0, -1, 1, -2, 2, -3, 3, 4):
            if dz == 0:
                deps = (own,)
            elif dz == 4:
                deps = (f"zb{h},1,{deep - 1}", f"zb{h},-1,{deep - 1}")
            else:
                sign = -1 if dz > 0 else 1
                deps = (f"zb{h},{sign},{abs(dz) - 1}",)
            for sign in (1, -1):
                for k in range(2):
                    if k == 1 and dz not in both_z[sign]:
                        continue
                    gather_piece(f"yb{h},{sign},{k},{dz}", PARTS["b"], dz, -sign * k, rows, rec_of(0, sign),
                                 deps if k == 0 else (f"yb{h},{sign},0,{dz}",), ("y", sign), (2, h, 1, k))
                    ends["b"].append(f"yb{h},{sign},{k},{dz}")
        for name in list(copies):
            if name.startswith((f"ya{h}", f"zb{h}")):
                ends[name[1]].append(name)

    def forward(name):
        start, count = PARTS[name]

        def run():
            for key in ends[name]:
                receive(key)

            def step(f, _):
                high, low = split(jnp.concatenate([rr[f], ri[f]], axis=0))
                w_high, w_low = split(gathered[f].reshape(NZ * NY * ROWS, 128))
                one = jnp.dot(high, jnp.concatenate([w_high, w_low], axis=1), preferred_element_type=F32)
                two = jnp.dot(low, w_high, preferred_element_type=F32)
                total = one[:, :128] + one[:, 128:] + two
                turned = pltpu.roll(total[ROWS:], 64, 1)
                made[f] = total[:ROWS] + jnp.where(low_half, -turned, turned)
                return _

            lax.fori_loop(start, start + count, step, 0)

        return run

    for name in PARTS:
        plan.add("fwd" + name, ends[name] + [f"w{h}in" for h in range(len(CHUNKS))], forward(name),
                 dur=6.0 * PARTS[name][1] / FL, rank=(3,))

    members = tuple(range(ROWS // 8))
    window_tasks(1, "v", members, lambda j: made.at[:, pl.ds(8 * j, 8), :], x2, y2,
                 lambda j: back.at[:, pl.ds(8 * j, 8), :], ("fwda", "fwdb"), (4,))

    order = plan.order()
    for name in order:
        plan.tasks[name][1]()
    out[...] = back[...]
    for value in copies.values():
        (value[0] if isinstance(value, tuple) else value).wait_send()
    for drain in waits:
        drain()
    kernel.plan = plan
    kernel.ordered = order


def iterate(response_real, response_imaginary, focus, onset, inv, fwd):
    chunks, nr = len(CHUNKS), CHUNKS[0][1]
    na, nb = SPLIT, FL - SPLIT
    vmem = pl.BlockSpec(memory_space=pltpu.VMEM)
    scratch = [
        pltpu.VMEM((FL, NZ, NY, ROWS, 128), F32),
        pltpu.VMEM((28 * chunks, na, nr, 128), F32),
        pltpu.VMEM((4 * chunks, na, nr, 128), F32),
        pltpu.VMEM((24 * chunks, nb, nr, 128), F32),
        pltpu.VMEM((8 * chunks, nb, nr, 128), F32),
        pltpu.VMEM((FL, NZ, NY, ROWS, 128), F32),
        pltpu.VMEM((FL, 2 * ROWS, 128), F32),
        pltpu.VMEM((NF * FL, 8, 128), F32),
        pltpu.VMEM((NF * FL, 8, 128), F32),
        pltpu.VMEM((NF * FL, 8, 128), F32),
        pltpu.VMEM((NF * FL, 8, 128), F32),
        pltpu.VMEM((FL, ROWS, 128), F32),
        pltpu.VMEM((FL, ROWS, 128), F32),
        pltpu.SemaphoreType.DMA((128 * chunks,)),
        pltpu.SemaphoreType.DMA((128 * chunks,)),
        pltpu.SemaphoreType.DMA((2, NF)),
        pltpu.SemaphoreType.DMA((2, NF)),
        pltpu.SemaphoreType.DMA((2, NF)),
        pltpu.SemaphoreType.DMA((2, NF)),
    ]
    return pl.pallas_call(
        kernel,
        out_shape=jax.ShapeDtypeStruct((FL, ROWS, 128), F32),
        in_specs=[vmem] * 6,
        out_specs=vmem,
        scratch_shapes=scratch,
        compiler_params=pltpu.CompilerParams(
            collective_id=0, has_side_effects=True, vmem_limit_bytes=60 * 1024 * 1024
        ),
    )(response_real, response_imaginary, focus, onset, inv, fwd)


def on_device(response_real, response_imaginary, focus, initial, onset):
    inv, fwd = dft_tables(NF * FL)
    pairs = onset.reshape(ROWS // 8, 4, 128)
    update = iterate(response_real, response_imaginary, focus, pairs, jnp.asarray(inv), jnp.asarray(fwd))
    return initial - jnp.transpose(update, (1, 0, 2))


def solution(mesh):
    in_specs = (
        P("freq", "rec", None),
        P("freq", "rec", None),
        P("rec", "freq", None),
        P("rec", "freq", None),
        P("rec", None),
    )
    return jax.shard_map(
        on_device, mesh=mesh, in_specs=in_specs, out_specs=P("rec", "freq", None), check_vma=False
    )
```

time: 390 us -> 165 us (0.42)
  waiting for transfers between devices: 241 us -> 0 us
  Pallas kernels: 0 us -> 159 us
  matrix products: 39.7 us -> 0 us
  blocking collectives: 38.4 us -> 0 us
  local copies, waits for them, and re-layouts: 36 us -> 3.21 us
  other arithmetic: 15.2 us -> 1.71 us
  between operations: 13.2 us -> 0.02 us
  starting transfers between devices: 5.78 us -> 0 us
    pallas_call x0 -> x1, Pallas kernels: none -> 159 us  [iterate(): pl.pallas_call(kernel, out_shape=jax.ShapeDtypeStruct((FL, ROWS, 128), F3...]
    unnamed x4 -> x0, waiting for transfers between devices: 109 us -> none
    all_gather x1 -> x0, waiting for transfers between devices: 101 us -> none  [iterate(): lax.all_gather(returned, REC, axis=0, tiled=True)]
    dot_general x8 -> x0, matrix products: 39.7 us -> none  [the longest x1 9.26 us: forward_terms(): jnp.einsum('frs,sfq->rfq', imag_part, values, precision=lax.Precision.HIG...]
    all_to_all x3 -> x0, blocking collectives: 38.4 us -> none  [the longest x1 13.5 us: iterate(): lax.all_to_all(forward, 'freq', split_axis=0, concat_axis=1, tiled=True)]
    reduce_scatter x1 -> x0, waiting for transfers between devices: 24.4 us -> none  [sum_by_axis(): total = lax.psum_scatter(total, axis, scatter_dimension=0, tiled=True)]
    unnamed x12 -> x3, local copies, waits for them, and re-layouts: 14.5 us -> 1.8 us
    all_to_all x6 -> x0, local copies, waits for them, and re-layouts: 7.57 us -> none  [the longest x2 2.52 us: iterate(): lax.all_to_all(windowed, 'freq', split_axis=1, concat_axis=0, tiled=True)]
  transfers between devices with their start and end apart: 4 -> 0, of which waited for: 4 -> 0; matrix products, arithmetic and copies ran while one was open for 1% -> 0% of each run, Pallas kernels for 0% -> 0%
where the time goes in v1:
time: 165 us; the launch traced here: 164 us
  Pallas kernels  159 us (96%)
  local copies, waits for them, and re-layouts  3.21 us (2%)
  other arithmetic  1.71 us (1%)
    pallas_call x1, Pallas kernels, iterate(): pl.pallas_call(kernel, out_shape=jax.ShapeDtypeStruct((FL, ROWS, 128), F3...  159 us

profile of v1, /device:TPU:1, one launch (start us, length us, event | category | flops | bytes accessed | tf_op | source)
XLA Modules:
  0.0 164.4 jit_solution(11097549916603424629)
XLA Ops:
  0.0 1.4 reshape.3.onset
  1.4 1.8 %copy.8.focus = f32[48,12,128]{2,1,0:T(8,128)} copy(f32[48,12,128]{2,0,1:T(8,128)} %param.9) | data formatting | bytes 589824 | tf_op args[2]
  3.2 0.0 copy-start
  3.2 159.4 %shard_map.73 = f32[12,48,128]{2,1,0:T(8,128)} custom-call(f32[12,48,1536]{2,1,0:T(8,128)} %rr.1, f32[12,48,1536]{2,1,0:T(8,128)} %ri.1, f32[48,12,128]{2,1,0:T(8,128)} %copy.8.focus, s32[6,4,128]{2,1,0:T(4,128)} %reshape.3.onset, bf16[192,576]{1,0:T(8,128)(2,1)} %constant.4.clone.inv, bf16[192,576]{1,0:T(8,128)(2,1)} %constant.5.clone.fwd), custom_call_target="tpu_custom_call" | custom-call | tf_op jit(solution)/shard_map/pallas_call | solution.py:486
  162.6 0.0 copy-done
  162.6 1.7 %bitcast_subtract_fusion = f32[48,12,128]{2,0,1:T(8,128)} fusion(f32[48,12,128]{2,0,1:T(8,128)S(1)} %copy-done, f32[12,48,128]{2,1,0:T(8,128)} %shard_map.73), kind=kLoop, calls=%fused_computation | loop fusion | flops 73728 | bytes 884736 | tf_op jit(solution)/shard_map/sub | solution.py:502
Async XLA Ops:
  3.2 159.4 %copy-start = (f32[48,12,128]{2,0,1:T(8,128)S(1)}, f32[48,12,128]{2,0,1:T(8,128)}, u32[]{:S(2)}) copy-start(f32[48,12,128]{2,0,1:T(8,128)} %param.10) | copy-start | bytes 884740

commit v2 on v1

--- a/solution.py
+++ b/solution.py
@@ -21,6 +21,7 @@
 CHUNKS = ((0, 24), (24, 24))
 RATE = 46.6e3
 LATENCY = 1.8
+BACKLOG = 2.0
 
 
 def split(value):
@@ -72,6 +73,8 @@
                 when = 0.0
                 for dep in deps:
                     when = max(when, arrived.get(dep, 1e9))
+                if link is not None:
+                    when = max(when, free.get(link, 0.0) - BACKLOG)
                 if when <= now:
                     ready.append((rank, name))
                 soonest = when if soonest is None else min(soonest, when)
@@ -97,7 +100,7 @@
 
 
 def kernel(rr, ri, focus, onset, inv, fwd, out, *scratch):
-    (part, stage_a1, stage_a2, stage_b1, stage_b2, gathered, xs, x1, y1, x2, y2, made, back,
+    (resp, load_sem, part, stage_a1, stage_a2, stage_b1, stage_b2, gathered, xs, x1, y1, x2, y2, made, back,
      send_sem, recv_sem, win_send, win_recv, ret_send, ret_recv) = scratch
     me_f, me_r = lax.axis_index("freq"), lax.axis_index("rec")
     z, y = lax.div(me_r, NY), lax.rem(me_r, NY)
@@ -110,6 +113,15 @@
 
     def rec_of(dz, dy):
         return at_z(dz) * NY + at_y(dy)
+
+    def load(c, f):
+        source = (rr, ri)[c]
+        return pltpu.make_async_copy(source.at[f], resp.at[f, pl.ds(ROWS * c, ROWS), :], load_sem.at[c, f])
+
+    for part_start, part_count in (PARTS["b"], PARTS["a"]):
+        for f in range(part_start, part_start + part_count):
+            load(0, f).start()
+            load(1, f).start()
 
     barrier = pltpu.get_barrier_semaphore()
     for dz, dy in ((1, 0), (-1, 0), (0, 1), (0, -1)):
@@ -131,7 +143,7 @@
         return copies[name]
 
     for f in range(FL):
-        value = focus[:, f, :]
+        value = focus[f]
         turned = pltpu.roll(value, 64, 1)
         xs[f, 0:ROWS, :] = value
         xs[f, ROWS : 2 * ROWS, :] = jnp.where(low_half, turned, -turned)
@@ -139,11 +151,13 @@
     def adjoint(start, count):
         def run():
             def step(f, _):
+                load(0, f).wait()
+                load(1, f).wait()
                 x_high, x_low = split(xs[f])
                 both = jnp.concatenate([x_high, x_low], axis=1)
                 for c in range(4):
                     cols = pl.ds(384 * c, 384)
-                    high, low = split(jnp.concatenate([rr[f, :, cols], ri[f, :, cols]], axis=0))
+                    high, low = split(resp[f, :, cols])
                     dims = (((0,), (0,)), ((), ()))
                     one = lax.dot_general(high, both, dims, preferred_element_type=F32)
                     two = lax.dot_general(low, x_high, dims, preferred_element_type=F32)
@@ -279,8 +293,8 @@
         spectrum = jnp.concatenate([jnp.concatenate(tops, axis=1), jnp.concatenate(bottoms, axis=1)], axis=0)
         high, low = split(spectrum)
         traces = jnp.dot(inv[...], jnp.concatenate([high, low, high], axis=0), preferred_element_type=F32)
-        limit = onset[jnp.minimum(me_f, ROWS // 8 - 1)]
-        limits = jnp.concatenate([limit[m : m + 1, :] for m in range(4)], axis=1)
+        limit = onset[pl.ds(pl.multiple_of(8 * jnp.minimum(me_f, ROWS // 8 - 1), 8), 8), :]
+        limits = jnp.concatenate([limit[m : m + 1, :] for m in range(8)], axis=1)
         sample = lax.broadcasted_iota(jnp.int32, traces.shape, 0)
         kept = jnp.where(sample < limits, traces, 0.0)
         high, low = split(kept)
@@ -425,7 +439,7 @@
                 receive(key)
 
             def step(f, _):
-                high, low = split(jnp.concatenate([rr[f], ri[f]], axis=0))
+                high, low = split(resp[f])
                 w_high, w_low = split(gathered[f].reshape(NZ * NY * ROWS, 128))
                 one = jnp.dot(high, jnp.concatenate([w_high, w_low], axis=1), preferred_element_type=F32)
                 two = jnp.dot(low, w_high, preferred_element_type=F32)
@@ -463,6 +477,8 @@
     na, nb = SPLIT, FL - SPLIT
     vmem = pl.BlockSpec(memory_space=pltpu.VMEM)
     scratch = [
+        pltpu.VMEM((FL, 2 * ROWS, response_real.shape[2]), F32),
+        pltpu.SemaphoreType.DMA((2, FL)),
         pltpu.VMEM((FL, NZ, NY, ROWS, 128), F32),
         pltpu.VMEM((28 * chunks, na, nr, 128), F32),
         pltpu.VMEM((4 * chunks, na, nr, 128), F32),
@@ -486,7 +502,7 @@
     return pl.pallas_call(
         kernel,
         out_shape=jax.ShapeDtypeStruct((FL, ROWS, 128), F32),
-        in_specs=[vmem] * 6,
+        in_specs=[pl.BlockSpec(memory_space=pl.ANY)] * 2 + [vmem] * 4,
         out_specs=vmem,
         scratch_shapes=scratch,
         compiler_params=pltpu.CompilerParams(
@@ -497,8 +513,8 @@
 
 def on_device(response_real, response_imaginary, focus, initial, onset):
     inv, fwd = dft_tables(NF * FL)
-    pairs = onset.reshape(ROWS // 8, 4, 128)
-    update = iterate(response_real, response_imaginary, focus, pairs, jnp.asarray(inv), jnp.asarray(fwd))
+    by_freq = jnp.transpose(focus, (1, 0, 2))
+    update = iterate(response_real, response_imaginary, by_freq, onset, jnp.asarray(inv), jnp.asarray(fwd))
     return initial - jnp.transpose(update, (1, 0, 2))
 
 

time: 165 us -> 147 us (0.89)
  Pallas kernels: 159 us -> 145 us
  local copies, waits for them, and re-layouts: 3.21 us -> 0.01 us
    pallas_call x1, Pallas kernels: 159 us -> 145 us  [iterate(): pl.pallas_call(kernel, out_shape=jax.ShapeDtypeStruct((FL, ROWS, 128), F3...]
    unnamed x3 -> x2, local copies, waits for them, and re-layouts: 1.8 us -> 0.01 us
where the time goes in v2:
time: 147 us; the launch traced here: 146 us
  Pallas kernels  145 us (99%)
  other arithmetic  1.71 us (1%)
    pallas_call x1, Pallas kernels, iterate(): pl.pallas_call(kernel, out_shape=jax.ShapeDtypeStruct((FL, ROWS, 128), F3...  145 us

profile of v2, /device:TPU:1, one launch (start us, length us, event | category | flops | bytes accessed | tf_op | source)
XLA Modules:
  0.0 146.5 jit_solution(6058720788429968685)
XLA Ops:
  0.0 0.0 copy-start
  0.0 144.7 %shard_map.73 = f32[12,48,128]{2,1,0:T(8,128)} custom-call(f32[12,48,1536]{2,1,0:T(8,128)} %rr.1, f32[12,48,1536]{2,1,0:T(8,128)} %ri.1, f32[12,48,128]{2,1,0:T(8,128)} %bitcast.3, s32[48,64]{1,0:T(8,128)} %onset.1, bf16[192,576]{1,0:T(8,128)(2,1)} %constant.4.clone.inv, bf16[192,576]{1,0:T(8,128)(2,1)} %constant.5.clone.fwd), custom_call_target="tpu_custom_call" | custom-call | tf_op jit(solution)/shard_map/pallas_call | solution.py:502
  144.7 0.0 copy-done
  144.8 1.7 %bitcast_subtract_fusion = f32[48,12,128]{2,0,1:T(8,128)} fusion(f32[48,12,128]{2,0,1:T(8,128)S(1)} %copy-done, f32[12,48,128]{2,1,0:T(8,128)} %shard_map.73), kind=kLoop, calls=%fused_computation | loop fusion | flops 73728 | bytes 884736 | tf_op jit(solution)/shard_map/sub | solution.py:518
Async XLA Ops:
  0.0 144.7 %copy-start = (f32[48,12,128]{2,0,1:T(8,128)S(1)}, f32[48,12,128]{2,0,1:T(8,128)}, u32[]{:S(2)}) copy-start(f32[48,12,128]{2,0,1:T(8,128)} %param.10) | copy-start | bytes 884740

commit v3 on v2

v3 whole, which is shorter than its diff:
```python
import functools
import heapq

import jax
import jax.numpy as jnp
import numpy as np
from jax import lax
from jax.experimental import pallas as pl
from jax.experimental.pallas import tpu as pltpu
from jax.sharding import PartitionSpec as P

MESH = pl.DeviceIdType.MESH
BF = jnp.bfloat16
F32 = jnp.float32

NF = 8
NZ, NY = 8, 4
FL = 12
ROWS = 48
SPLIT = 5
CHUNKS = 2
NR = ROWS // CHUNKS
COLS = NZ * NY * NR
MEMBERS = NR // 8
RATE = 46.6e3
LATENCY = 1.8
BACKLOG = 2.0


def split(value):
    high = value.astype(BF)
    low = (value - high.astype(F32)).astype(BF)
    return high, low


def dft_tables(freqs):
    samples = 2 * freqs
    phase = np.arange(freqs)[:, None] * np.arange(samples)[None, :] % samples
    angle = 2.0 * np.pi / samples * phase
    cosine, sine = np.cos(angle), np.sin(angle)
    factor = np.where(np.arange(freqs) == 0, 1.0, 2.0)[:, None] / samples
    inverse = np.concatenate([factor * cosine, -factor * sine]).T
    forward = np.concatenate([cosine, -sine])
    out = []
    for table in (inverse, forward):
        table = table.astype(np.float32)
        high = table.astype(jnp.bfloat16)
        low = (table - high.astype(np.float32)).astype(jnp.bfloat16)
        out.append(np.concatenate([high, high, low], axis=1))
    return out


PARTS = {"a": (0, SPLIT), "b": (SPLIT, FL - SPLIT)}


def halves(part, sign):
    start, count = PARTS[part]
    first = (count + 1) // 2 if part == "a" else count // 2
    return (start, first) if sign > 0 else (start + first, count - first)


class Plan:
    def __init__(self):
        self.tasks, self.sent = {}, {}

    def add(self, name, deps, run, link=None, size=0, dur=0.1, rank=(0,)):
        self.tasks[name] = (tuple(deps), run, link, size, dur, rank)

    def order(self):
        free, arrived, done = {}, {}, {}
        left = dict(self.tasks)
        now, order = 0.0, []
        while left:
            ready, soonest = [], None
            for name, (deps, run, link, size, dur, rank) in left.items():
                when = 0.0
                for dep in deps:
                    when = max(when, arrived.get(dep, 1e9))
                if link is not None:
                    when = max(when, free.get(link, 0.0) - BACKLOG)
                if when <= now:
                    ready.append((rank, name))
                soonest = when if soonest is None else min(soonest, when)
            if not ready:
                if soonest >= 1e9:
                    raise ValueError("cycle")
                now = soonest
                continue
            _, name = min(ready)
            deps, run, link, size, dur, rank = left.pop(name)
            now += dur
            order.append((now, name))
            if link is None:
                arrived[name] = now
            else:
                start = max(now, free.get(link, 0.0))
                free[link] = start + size / RATE
                arrived[name] = free[link] + LATENCY
                self.sent[name] = free[link]
            done[name] = now
        self.finish = now
        self.times = arrived
        return order


def kernel(rr, ri, focus_in, onset_in, inv_in, fwd_in, out, *scratch):
    (focus, onset, inv, fwd, small_sem, resp, load_sem, part, stage_a1, stage_a2, stage_b1, stage_b2, gathered, xs, x1, y1, x2, y2, acc, made, back,
     onset_own, onset_send, onset_recv, send_sem, recv_sem, win_send, win_recv, ret_send, ret_recv) = scratch
    me_f, me_r = lax.axis_index("freq"), lax.axis_index("rec")
    z, y = lax.div(me_r, NY), lax.rem(me_r, NY)

    def at_z(d):
        return lax.rem(z + (d + NZ), NZ) if d else z

    def at_y(d):
        return lax.rem(y + (d + NY), NY) if d else y

    def rec_of(dz, dy):
        return at_z(dz) * NY + at_y(dy)

    def load(c, h, name):
        start, count = PARTS[name]
        cols, freqs = pl.ds(COLS * h, COLS), pl.ds(start, count)
        return pltpu.make_async_copy(
            (rr, ri)[c].at[freqs, :, cols], resp.at[freqs, pl.ds(ROWS * c, ROWS), cols],
            load_sem.at[c, h, list(PARTS).index(name)])

    small = [pltpu.make_async_copy(src, dst, small_sem.at[i]) for i, (src, dst) in enumerate(
        ((focus_in, focus), (onset_in, onset), (inv_in, inv), (fwd_in, fwd)))]
    small[0].start()
    for h in range(CHUNKS):
        for name in PARTS:
            load(0, h, name).start()
            load(1, h, name).start()
        if h == 0:
            for copy in small[1:]:
                copy.start()

    barrier = pltpu.get_barrier_semaphore()
    for dz, dy in ((1, 0), (-1, 0), (0, 1), (0, -1)):
        pl.semaphore_signal(barrier, inc=1, device_id=(me_f, rec_of(dz, dy)), device_id_type=MESH)
    for d in range(1, NF):
        pl.semaphore_signal(barrier, inc=1, device_id=(lax.rem(me_f + d, NF), me_r), device_id_type=MESH)

    def onset_source(h):
        return lax.div(h * NZ * NY + me_r, CHUNKS)

    def onset_copy(u):
        index = me_r * CHUNKS + u
        target, h = lax.rem(index, NZ * NY), lax.div(index, NZ * NY)
        rows = onset.at[pl.ds(NR * u, NR), :]
        return target, h, rows, pltpu.make_async_remote_copy(
            src_ref=rows, dst_ref=onset_own.at[h], send_sem=onset_send.at[u], recv_sem=onset_recv.at[h],
            device_id=(me_f, target), device_id_type=MESH)

    for h in range(CHUNKS):
        @pl.when(onset_source(h) != me_r)
        def _():
            pl.semaphore_signal(barrier, inc=1, device_id=(me_f, onset_source(h)), device_id_type=MESH)

    def enter():
        for copy in small[1:]:
            copy.wait()
        peers = 4 + NF - 1
        for u in range(CHUNKS):
            peers += jnp.where(lax.rem(me_r * CHUNKS + u, NZ * NY) != me_r, 1, 0)
        pl.semaphore_wait(barrier, peers)
        for u in range(CHUNKS):
            target, h, rows, copy = onset_copy(u)

            @pl.when(target != me_r)
            def _():
                copy.start()

            @pl.when(target == me_r)
            def _():
                onset_own[h] = rows[...]

    def onset_ready():
        for u in range(CHUNKS):
            target, _h, _rows, copy = onset_copy(u)

            @pl.when(target != me_r)
            def _():
                copy.wait_send()

        for h in range(CHUNKS):
            @pl.when(onset_source(h) != me_r)
            def _():
                pltpu.make_async_remote_copy(
                    src_ref=onset_own.at[h], dst_ref=onset_own.at[h], send_sem=onset_send.at[0],
                    recv_sem=onset_recv.at[h], device_id=(me_f, me_r), device_id_type=MESH).wait_recv()

    lane = lax.broadcasted_iota(jnp.int32, (ROWS, 128), 1)
    low_half = lane < 64
    plan = Plan()
    copies = {}

    used = {}

    def piece(name, src, dst, target, phase, h):
        bank = h if phase == 0 else (CHUNKS + h if h < CHUNKS - 1 else 0)
        index = used[phase, h] = used.get((phase, h), -1) + 1
        copies[name] = pltpu.make_async_remote_copy(
            src_ref=src, dst_ref=dst, send_sem=send_sem.at[phase], recv_sem=recv_sem.at[bank, index],
            device_id=(me_f, target), device_id_type=MESH)
        return copies[name]

    small[0].wait()
    for f in range(FL):
        value = focus[f]
        turned = pltpu.roll(value, 64, 1)
        xs[f, 0:ROWS, :] = value
        xs[f, ROWS : 2 * ROWS, :] = jnp.where(low_half, turned, -turned)

    def adjoint(freqs, h, name):
        def run():
            if freqs[0] == PARTS[name][0]:
                load(0, h, name).wait()
                load(1, h, name).wait()

            def step(f, _):
                x_high, x_low = split(xs[f])
                left = jnp.concatenate([x_high, x_high], axis=0)
                right = jnp.concatenate([x_low, jnp.zeros_like(x_low)], axis=0)
                both = jnp.concatenate([left, right], axis=1)
                for c in range(2):
                    high, low = split(resp[f, :, pl.ds(COLS * h + COLS // 2 * c, COLS // 2)])
                    terms = lax.dot_general(jnp.concatenate([high, low], axis=0), both, (((0,), (0,)), ((), ())),
                                            preferred_element_type=F32)
                    total = terms[:, :128] + terms[:, 128:]
                    part[f, h, NZ // 2 * c : NZ // 2 * (c + 1)] = total.reshape(NZ // 2, NY, NR, 128)
                return _

            for f in freqs:
                step(f, 0)

        return run

    def groups(name, size):
        start, count = PARTS[name]
        return [tuple(range(f, min(f + size, start + count))) for f in range(start, start + count, size)]

    adjoint_done = {}
    for h in range(CHUNKS):
        for name in ("a", "b"):
            adjoint_done[h, name] = []
            for place, freqs in enumerate(groups(name, FL if h == 0 else 3)):
                key = f"adj{name}{h},{place}"
                adjoint_done[h, name].append(key)
                plan.add(key, (), adjoint(freqs, h, name), dur=3.4 / CHUNKS * len(freqs) / FL, rank=(0 if h == 0 else 1, max(h - 1, 0), 9, name != "a", place))

    slot = {"a1": 0, "a2": 0, "b1": 0, "b2": 0}
    stages = {"a1": stage_a1, "a2": stage_a2, "b1": stage_b1, "b2": stage_b2}

    def staging(kind, count):
        index = slot[kind]
        slot[kind] += 1
        return stages[kind].at[index, pl.ds(0, count)]

    def reduce_piece(name, kind, freqs, dz, dy, h, target, adds, deps, link, rank):
        start, count = freqs
        src = part.at[pl.ds(start, count), h, at_z(dz), at_y(dy)]
        dst = staging(kind, count)
        copy = piece(name, src, dst, target, 0, h)
        copies[name] = (copy, dst, start, count)

        def run():
            take(adds, dz, dy, h)
            copy.start()

        plan.add(name, tuple(adds) + tuple(deps), run, link, count * NR * 512, 0.12, rank)

    def take(adds, dz, dy, h):
        for other in adds:
            copy, dst, start, count = copies[other]
            copy.wait_recv()
            where = (pl.ds(start, count), h, at_z(dz), at_y(dy))
            part[where] += dst[...]

    for h in range(CHUNKS):
        deep = NZ // 2
        order_y = (2, 1, -1, 0)
        order_z = (4, 3, -3, 2, -2, 1, -1, 0)
        both_y = {1: (2, 0), -1: (1, -1)}
        both_z = {1: (4, 2, -2, 0), -1: (3, -3, 1, -1)}
        for k in range(deep, 0, -1):
            for place, dy in enumerate(order_y):
                for sign in (1, -1):
                    if k == deep and dy not in both_y[sign]:
                        continue
                    adds = [f"a1{h},{sign},{k + 1},{dy}"] if (k < deep - 1 or (k == deep - 1 and dy in both_y[sign])) else []
                    reduce_piece(f"a1{h},{sign},{k},{dy}", "a1", PARTS["a"], sign * k, dy, h, rec_of(sign, 0), adds,
                                 adjoint_done[h, "a"], ("z", sign), (1, h, 0, -k, place))
        for k in (2, 1):
            for place, dz in enumerate(order_z):
                for sign in (1, -1):
                    if k == 2 and dz not in both_z[sign]:
                        continue
                    adds = [f"b1{h},{sign},2,{dz}"] if k == 1 and dz in both_z[sign] else []
                    reduce_piece(f"b1{h},{sign},{k},{dz}", "b1", PARTS["b"], dz, sign * k, h, rec_of(0, sign), adds,
                                 adjoint_done[h, "b"], ("y", sign), (1, h, 0, -k, place))

        def first_sum(name, kind, d):
            keys = [f"{kind}{h},{sign},1,{d}" for sign in (1, -1)]

            def run(keys=keys, d=d, h=h, kind=kind):
                dz, dy = (0, d) if kind == "a1" else (d, 0)
                take(keys, dz, dy, h)

            plan.add(name, keys, run, dur=0.12, rank=(0, h, 0))

        for dy in order_y:
            first_sum(f"as{h},{dy}", "a1", dy)
        for dz in order_z:
            first_sum(f"bs{h},{dz}", "b1", dz)
        for sign in (1, -1):
            reduce_piece(f"a2{h},{sign},2", "a2", halves("a", sign), 0, 2 * sign, h, rec_of(0, sign), [],
                         (f"as{h},2",), ("y", sign), (0, h, 1, -2))
            reduce_piece(f"a2{h},{sign},1", "a2", PARTS["a"], 0, sign, h, rec_of(0, sign), [f"a2{h},{sign},2"],
                         (f"as{h},{sign}",), ("y", sign), (0, h, 1, -1))
            for k in range(deep, 0, -1):
                freqs = halves("b", sign) if k == deep else PARTS["b"]
                adds = [] if k == deep else [f"b2{h},{sign},{k + 1}"]
                source = 4 if k == deep else sign * k
                reduce_piece(f"b2{h},{sign},{k}", "b2", freqs, sign * k, 0, h, rec_of(sign, 0), adds,
                             (f"bs{h},{source}",), ("z", sign), (0, h, 1, -k))

        own_keys = [f"a2{h},{sign},1" for sign in (1, -1)] + [f"b2{h},{sign},1" for sign in (1, -1)]

        def own_sum(keys=tuple(own_keys), h=h):
            take(keys, 0, 0, h)

        plan.add(f"own{h}", own_keys + [f"as{h},0", f"bs{h},0"], own_sum, dur=0.2, rank=(0, h, 0))

    def block_of(buffer, h, j):
        return buffer.at[:, h, z, y, pl.ds(8 * (j - MEMBERS * h), 8), :]

    def out_copy(source, freqs, landing, which, j):
        start, count = freqs
        return pltpu.make_async_remote_copy(
            src_ref=source(j).at[pl.ds(start, count)], dst_ref=landing.at[pl.ds(FL * me_f + start, count)],
            send_sem=win_send.at[which, j], recv_sem=win_recv.at[which, me_f],
            device_id=(j, me_r), device_id_type=MESH)

    def in_wait(landing, freqs, which, sender):
        start, count = freqs
        where = landing.at[pl.ds(FL * sender + start, count)]
        pltpu.make_async_remote_copy(
            src_ref=where, dst_ref=where,
            send_sem=win_send.at[which, 0], recv_sem=win_recv.at[which, sender],
            device_id=(sender, me_r), device_id_type=MESH).wait_recv()

    def return_copy(clipped, target, which, d):
        return pltpu.make_async_remote_copy(
            src_ref=clipped.at[pl.ds(FL * d, FL)], dst_ref=target(me_f),
            send_sem=ret_send.at[which, d], recv_sem=ret_recv.at[which, me_f],
            device_id=(d, me_r), device_id_type=MESH)

    def return_wait(target, which, j):
        pltpu.make_async_remote_copy(
            src_ref=target(j), dst_ref=target(j), send_sem=ret_send.at[which, 0],
            recv_sem=ret_recv.at[which, j], device_id=(j, me_r), device_id_type=MESH).wait_recv()

    def window(landing, clipped, starts):
        half = lax.broadcasted_iota(jnp.int32, (NF * FL, 128), 1) < 64
        tops, bottoms = [], []
        for m in range(4):
            first, second = landing[:, 2 * m, :], landing[:, 2 * m + 1, :]
            tops.append(jnp.where(half, first, pltpu.roll(second, 64, 1)))
            bottoms.append(jnp.where(half, pltpu.roll(first, 64, 1), second))
        spectrum = jnp.concatenate([jnp.concatenate(tops, axis=1), jnp.concatenate(bottoms, axis=1)], axis=0)
        high, low = split(spectrum)
        traces = jnp.dot(inv[...], jnp.concatenate([high, low, high], axis=0), preferred_element_type=F32)
        limit = starts()
        limits = jnp.concatenate([limit[m : m + 1, :] for m in range(8)], axis=1)
        sample = lax.broadcasted_iota(jnp.int32, traces.shape, 0)
        kept = jnp.where(sample < limits, traces, 0.0)
        high, low = split(kept)
        again = jnp.dot(fwd[...], jnp.concatenate([high, low, high], axis=0), preferred_element_type=F32)
        for m in range(4):
            real = again[: NF * FL, 128 * m : 128 * m + 128]
            imag = again[NF * FL :, 128 * m : 128 * m + 128]
            clipped[:, 2 * m, :] = jnp.where(half, real, pltpu.roll(imag, 64, 1))
            clipped[:, 2 * m + 1, :] = jnp.where(half, pltpu.roll(real, 64, 1), imag)

    def window_tasks(which, tag, members, source, sends, landing, clipped, starts, target, rank):
        inside = (me_f >= members[0]) & (me_f <= members[-1])

        def scatter(freqs, row):
            def run():
                for j in members:
                    @pl.when(me_f != j)
                    def _():
                        out_copy(source, freqs, landing, row, j).start()

                    @pl.when(me_f == j)
                    def _():
                        start, count = freqs
                        landing[FL * j + start : FL * j + start + count] = source(j)[start : start + count]

            return run

        def apply():
            @pl.when(inside)
            def _():
                for sender in range(NF):
                    @pl.when(me_f != sender)
                    def _():
                        for freqs, row, _deps in sends:
                            in_wait(landing, freqs, row, sender)

                window(landing, clipped, starts)
                for d in range(NF):
                    @pl.when(me_f != d)
                    def _():
                        return_copy(clipped, target, which, d).start()

                target(me_f)[...] = clipped[pl.ds(FL * me_f, FL)]

        def collect():
            if which == 1:
                drain()
            for j in members:
                @pl.when(me_f != j)
                def _():
                    return_wait(target, which, j)

        def drain():
            for j in members:
                @pl.when(me_f != j)
                def _():
                    for freqs, row, _deps in sends:
                        out_copy(source, freqs, landing, row, j).wait_send()

            @pl.when(inside)
            def _():
                for d in range(NF):
                    @pl.when(me_f != d)
                    def _():
                        return_copy(clipped, target, which, d).wait_send()

        if which == 0:
            plan.add(tag + "drain", (tag + "in",) + ("w1in",), drain, dur=0.3, rank=(5,))
        outs = []
        for freqs, row, deps in sends:
            outs.append(f"{tag}out{row}")
            plan.add(outs[-1], deps, scatter(freqs, row), ("x", 0), len(members) * 8 * freqs[1] * 340, 0.2, rank)
        plan.add(tag + "win", outs, apply, ("x", 1), len(members) * 8 * FL * 340, 1.5, rank)
        plan.add(tag + "in", (tag + "win",), collect, dur=0.2, rank=rank)

    def onset_here():
        return onset[pl.ds(pl.multiple_of(8 * jnp.minimum(me_f, ROWS // 8 - 1), 8), 8), :]

    plan.add("onset", ("own0",), onset_ready, dur=0.05, rank=(0, 0, 0))
    for h in range(CHUNKS):
        def onset_summed(h=h):
            j = jnp.clip(me_f - MEMBERS * h, 0, MEMBERS - 1)
            return onset_own[h, pl.ds(pl.multiple_of(8 * j, 8), 8), :]

        members = tuple(range(MEMBERS * h, MEMBERS * h + MEMBERS))
        window_tasks(0, f"w{h}", members, functools.partial(block_of, part, h),
                     [((0, FL), 0, (f"own{h}", "onset"))], x1, y1, onset_summed,
                     functools.partial(block_of, gathered, h), (0, h, 0))

    def gather_piece(name, freqs, dz, dy, h, target, deps, link, rank):
        start, count = freqs
        where = gathered.at[pl.ds(start, count), h, at_z(dz), at_y(dy)]
        copy = piece(name, where, where, target, 1, h)
        arrivals = [dep for dep in deps if dep in copies]

        def run():
            for dep in arrivals:
                receive(dep)
            copy.start()

        plan.add(name, deps, run, link, count * NR * 512, 0.08, rank)

    received = set()

    def receive(name):
        if name not in received:
            received.add(name)
            copies[name].wait_recv()

    ends = {(h, name): [] for h in range(CHUNKS) for name in PARTS}
    for h in range(CHUNKS):
        own = f"w{h}in"
        deep = NZ // 2
        for sign in (1, -1):
            gather_piece(f"ya{h},{sign},0", PARTS["a"], 0, 0, h, rec_of(0, sign), (own,), ("y", sign), (2, h, 0))
            gather_piece(f"zb{h},{sign},0", PARTS["b"], 0, 0, h, rec_of(sign, 0), (own,), ("z", sign), (2, h, 0))
        for sign in (1, -1):
            gather_piece(f"ya{h},{sign},1", halves("a", sign), 0, -sign, h, rec_of(0, sign), (f"ya{h},{sign},0",),
                         ("y", sign), (2, h, 0))
            for k in range(1, deep):
                freqs = halves("b", sign) if k == deep - 1 else PARTS["b"]
                gather_piece(f"zb{h},{sign},{k}", freqs, -sign * k, 0, h, rec_of(sign, 0), (f"zb{h},{sign},{k - 1}",),
                             ("z", sign), (2, h, 0))
        for dy in (0, -1, 1, 2):
            if dy == 0:
                deps = (own,)
            elif dy == 2:
                deps = (f"ya{h},1,1", f"ya{h},-1,1")
            else:
                deps = (f"ya{h},{-dy},0",)
            for sign in (1, -1):
                for k in range(deep):
                    if k == deep - 1 and dy not in both_y[sign]:
                        continue
                    gather_piece(f"za{h},{sign},{k},{dy}", PARTS["a"], -sign * k, dy, h, rec_of(sign, 0),
                                 deps if k == 0 else (f"za{h},{sign},{k - 1},{dy}",), ("z", sign), (2, h, 1, k))
                    ends[h, "a"].append(f"za{h},{sign},{k},{dy}")
        for dz in (0, -1, 1, -2, 2, -3, 3, 4):
            if dz == 0:
                deps = (own,)
            elif dz == 4:
                deps = (f"zb{h},1,{deep - 1}", f"zb{h},-1,{deep - 1}")
            else:
                sign = -1 if dz > 0 else 1
                deps = (f"zb{h},{sign},{abs(dz) - 1}",)
            for sign in (1, -1):
                for k in range(2):
                    if k == 1 and dz not in both_z[sign]:
                        continue
                    gather_piece(f"yb{h},{sign},{k},{dz}", PARTS["b"], dz, -sign * k, h, rec_of(0, sign),
                                 deps if k == 0 else (f"yb{h},{sign},0,{dz}",), ("y", sign), (2, h, 1, k))
                    ends[h, "b"].append(f"yb{h},{sign},{k},{dz}")
        for name in list(copies):
            if name.startswith((f"ya{h}", f"zb{h}")):
                ends[h, name[1]].append(name)

    def forward(freqs, h, name):
        def run():
            for key in ends[h, name]:
                receive(key)

            def step(f, _):
                high, low = split(resp[f, :, pl.ds(COLS * h, COLS)])
                w_high, w_low = split(gathered[f, h].reshape(COLS, 128))
                terms = jnp.dot(jnp.concatenate([high, low], axis=0), jnp.concatenate([w_high, w_low], axis=1),
                                preferred_element_type=F32)
                total = terms[: 2 * ROWS, :128] + terms[: 2 * ROWS, 128:] + terms[2 * ROWS :, :128]
                if h > 0:
                    total = total + acc[f]
                if h < CHUNKS - 1:
                    acc[f] = total
                else:
                    turned = pltpu.roll(total[ROWS:], 64, 1)
                    made[f] = total[:ROWS] + jnp.where(low_half, -turned, turned)
                return _

            for f in freqs:
                step(f, 0)

        return run

    last = {}
    for h in range(CHUNKS):
        for name in PARTS:
            last[name] = []
            for place, freqs in enumerate(groups(name, 3 if h < CHUNKS - 1 else FL)):
                key = f"fwd{name}{h},{place}"
                last[name].append(key)
                before = [f"fwd{name}{h - 1},{p}" for p in range(len(groups(name, 3)))] if h else []
                plan.add(key, ends[h, name] + [f"w{h}in"] + before, forward(freqs, h, name),
                         dur=3.4 / CHUNKS * len(freqs) / FL, rank=(3, h))

    window_tasks(1, "v", tuple(range(ROWS // 8)), lambda j: made.at[:, pl.ds(8 * j, 8), :],
                 [(PARTS[name], 1 + place, last[name]) for place, name in enumerate(("b", "a"))], x2, y2, onset_here,
                 lambda j: back.at[:, pl.ds(8 * j, 8), :], (4,))

    order = plan.order()
    entered = False
    for _now, name in order:
        if plan.tasks[name][2] and not entered:
            enter()
            entered = True
        plan.tasks[name][1]()
    blocks = CHUNKS * FL * (NZ * NY - 1)
    for phase, buffer in enumerate((part, gathered)):
        amount = buffer.reshape(CHUNKS * FL * NZ * NY, NR, 128).at[pl.ds(0, blocks)]
        pltpu.make_async_copy(amount, amount, send_sem.at[phase]).wait()
    out[...] = back[...]
    kernel.plan = plan
    kernel.ordered = order


def iterate(response_real, response_imaginary, focus, onset, inv, fwd):
    na, nb = SPLIT, FL - SPLIT
    vmem = pl.BlockSpec(memory_space=pltpu.VMEM)
    scratch = [
        pltpu.VMEM(focus.shape, F32),
        pltpu.VMEM(onset.shape, jnp.int32),
        pltpu.VMEM(inv.shape, BF),
        pltpu.VMEM(fwd.shape, BF),
        pltpu.SemaphoreType.DMA((4,)),
        pltpu.VMEM((FL, 2 * ROWS, response_real.shape[2]), F32),
        pltpu.SemaphoreType.DMA((2, CHUNKS, 2)),
        pltpu.VMEM((FL, CHUNKS, NZ, NY, NR, 128), F32),
        pltpu.VMEM((28 * CHUNKS, na, NR, 128), F32),
        pltpu.VMEM((4 * CHUNKS, na, NR, 128), F32),
        pltpu.VMEM((24 * CHUNKS, nb, NR, 128), F32),
        pltpu.VMEM((8 * CHUNKS, nb, NR, 128), F32),
        pltpu.VMEM((FL, CHUNKS, NZ, NY, NR, 128), F32),
        pltpu.VMEM((FL, 2 * ROWS, 128), F32),
        pltpu.VMEM((NF * FL, 8, 128), F32),
        pltpu.VMEM((NF * FL, 8, 128), F32),
        pltpu.VMEM((NF * FL, 8, 128), F32),
        pltpu.VMEM((NF * FL, 8, 128), F32),
        pltpu.VMEM((FL, 2 * ROWS, 128), F32),
        pltpu.VMEM((FL, ROWS, 128), F32),
        pltpu.VMEM((FL, ROWS, 128), F32),
        pltpu.VMEM((CHUNKS, NR, onset.shape[1]), jnp.int32),
        pltpu.SemaphoreType.DMA((CHUNKS,)),
        pltpu.SemaphoreType.DMA((CHUNKS,)),
        pltpu.SemaphoreType.DMA((2,)),
        pltpu.SemaphoreType.DMA((2 * CHUNKS - 1, 64)),
        pltpu.SemaphoreType.DMA((3, NF)),
        pltpu.SemaphoreType.DMA((3, NF)),
        pltpu.SemaphoreType.DMA((2, NF)),
        pltpu.SemaphoreType.DMA((2, NF)),
    ]
    return pl.pallas_call(
        kernel,
        out_shape=jax.ShapeDtypeStruct((FL, ROWS, 128), F32),
        in_specs=[pl.BlockSpec(memory_space=pl.ANY)] * 6,
        out_specs=vmem,
        scratch_shapes=scratch,
        compiler_params=pltpu.CompilerParams(
            collective_id=0, has_side_effects=True, vmem_limit_bytes=60 * 1024 * 1024
        ),
    )(response_real, response_imaginary, focus, onset, inv, fwd)


def on_device(response_real, response_imaginary, focus, initial, onset):
    inv, fwd = dft_tables(NF * FL)
    by_freq = jnp.transpose(focus, (1, 0, 2))
    update = iterate(response_real, response_imaginary, by_freq, onset, jnp.asarray(inv), jnp.asarray(fwd))
    return initial - jnp.transpose(update, (1, 0, 2))


def solution(mesh):
    in_specs = (
        P("freq", "rec", None),
        P("freq", "rec", None),
        P("rec", "freq", None),
        P("rec", "freq", None),
        P("rec", None),
    )
    return jax.shard_map(
        on_device, mesh=mesh, in_specs=in_specs, out_specs=P("rec", "freq", None), check_vma=False
    )
```

time: 147 us -> 136 us (0.925)
  Pallas kernels: 145 us -> 134 us
    pallas_call x1, Pallas kernels: 145 us -> 134 us  [iterate(): pl.pallas_call(kernel, out_shape=jax.ShapeDtypeStruct((FL, ROWS, 128), F3...]
where the time goes in v3:
time: 136 us
  Pallas kernels  134 us (99%)
  other arithmetic  1.71 us (1%)
    pallas_call x1, Pallas kernels, iterate(): pl.pallas_call(kernel, out_shape=jax.ShapeDtypeStruct((FL, ROWS, 128), F3...  134 us

profile of v3, /device:TPU:1, one launch (start us, length us, event | category | flops | bytes accessed | tf_op | source)
XLA Modules:
  0.0 135.6 jit_solution(1767200879468438351)
XLA Ops:
  0.0 0.0 copy-start
  0.0 133.9 %shard_map.73 = f32[12,48,128]{2,1,0:T(8,128)} custom-call(f32[12,48,1536]{2,1,0:T(8,128)} %rr.1, f32[12,48,1536]{2,1,0:T(8,128)} %ri.1, f32[12,48,128]{2,1,0:T(8,128)} %bitcast.3, s32[48,64]{1,0:T(8,128)} %onset_in.1, bf16[192,576]{1,0:T(8,128)(2,1)} %constant.4.clone.inv_in, bf16[192,576]{1,0:T(8,128)(2,1)} %constant.5.clone.fwd_in), custom_call_target="tpu_custom_call" | custom-call | tf_op jit(solution)/shard_map/pallas_call | solution.py:624
  133.9 0.0 copy-done
  133.9 1.7 %bitcast_subtract_fusion = f32[48,12,128]{2,0,1:T(8,128)} fusion(f32[48,12,128]{2,0,1:T(8,128)S(1)} %copy-done, f32[12,48,128]{2,1,0:T(8,128)} %shard_map.73), kind=kLoop, calls=%fused_computation | loop fusion | flops 73728 | bytes 884736 | tf_op jit(solution)/shard_map/sub | solution.py:640
Async XLA Ops:
  0.0 133.9 %copy-start = (f32[48,12,128]{2,0,1:T(8,128)S(1)}, f32[48,12,128]{2,0,1:T(8,128)}, u32[]{:S(2)}) copy-start(f32[48,12,128]{2,0,1:T(8,128)} %param.10) | copy-start | bytes 884740

commit v4 on v3

--- a/solution.py
+++ b/solution.py
@@ -24,7 +24,9 @@
 MEMBERS = NR // 8
 RATE = 46.6e3
 LATENCY = 1.8
-BACKLOG = 2.0
+ADJ, FWD = 0, 0
+X_LATENCY = 4.0
+BACKLOG = 1.0
 
 
 def split(value):
@@ -95,7 +97,7 @@
             else:
                 start = max(now, free.get(link, 0.0))
                 free[link] = start + size / RATE
-                arrived[name] = free[link] + LATENCY
+                arrived[name] = free[link] + (LATENCY if link[0] != "x" else X_LATENCY)
                 self.sent[name] = free[link]
             done[name] = now
         self.finish = now
@@ -103,8 +105,8 @@
         return order
 
 
-def kernel(rr, ri, focus_in, onset_in, inv_in, fwd_in, out, *scratch):
-    (focus, onset, inv, fwd, small_sem, resp, load_sem, part, stage_a1, stage_a2, stage_b1, stage_b2, gathered, xs, x1, y1, x2, y2, acc, made, back,
+def kernel(rr, ri, focus_in, onset_in, inv_in, fwd_in, initial_in, out, *scratch):
+    (focus, onset, inv, fwd, initial, small_sem, resp, load_sem, part, stage_a1, stage_a2, stage_b1, stage_b2, gathered, xs, x1, y1, x2, y2, acc, made, back,
      onset_own, onset_send, onset_recv, send_sem, recv_sem, win_send, win_recv, ret_send, ret_recv) = scratch
     me_f, me_r = lax.axis_index("freq"), lax.axis_index("rec")
     z, y = lax.div(me_r, NY), lax.rem(me_r, NY)
@@ -126,7 +128,7 @@
             load_sem.at[c, h, list(PARTS).index(name)])
 
     small = [pltpu.make_async_copy(src, dst, small_sem.at[i]) for i, (src, dst) in enumerate(
-        ((focus_in, focus), (onset_in, onset), (inv_in, inv), (fwd_in, fwd)))]
+        ((focus_in, focus), (onset_in, onset), (inv_in, inv), (fwd_in, fwd), (initial_in, initial)))]
     small[0].start()
     for h in range(CHUNKS):
         for name in PARTS:
@@ -205,6 +207,20 @@
             src_ref=src, dst_ref=dst, send_sem=send_sem.at[phase], recv_sem=recv_sem.at[bank, index],
             device_id=(me_f, target), device_id_type=MESH)
         return copies[name]
+
+    def each(freqs, step, together):
+        whole = len(freqs) // together * together if together else 0
+        if whole > together:
+            def body(i, carry):
+                for k in range(together):
+                    step(freqs[0] + i * together + k, 0)
+                return carry
+
+            lax.fori_loop(0, whole // together, body, 0)
+        else:
+            whole = 0
+        for f in freqs[whole:]:
+            step(f, 0)
 
     small[0].wait()
     for f in range(FL):
@@ -232,8 +248,7 @@
                     part[f, h, NZ // 2 * c : NZ // 2 * (c + 1)] = total.reshape(NZ // 2, NY, NR, 128)
                 return _
 
-            for f in freqs:
-                step(f, 0)
+            each(freqs, step, ADJ)
 
         return run
 
@@ -336,31 +351,20 @@
     def block_of(buffer, h, j):
         return buffer.at[:, h, z, y, pl.ds(8 * (j - MEMBERS * h), 8), :]
 
-    def out_copy(source, freqs, landing, which, j):
+    def out_copy(source, freqs, landing, row, j):
         start, count = freqs
         return pltpu.make_async_remote_copy(
             src_ref=source(j).at[pl.ds(start, count)], dst_ref=landing.at[pl.ds(FL * me_f + start, count)],
-            send_sem=win_send.at[which, j], recv_sem=win_recv.at[which, me_f],
-            device_id=(j, me_r), device_id_type=MESH)
-
-    def in_wait(landing, freqs, which, sender):
-        start, count = freqs
-        where = landing.at[pl.ds(FL * sender + start, count)]
-        pltpu.make_async_remote_copy(
-            src_ref=where, dst_ref=where,
-            send_sem=win_send.at[which, 0], recv_sem=win_recv.at[which, sender],
-            device_id=(sender, me_r), device_id_type=MESH).wait_recv()
-
-    def return_copy(clipped, target, which, d):
+            send_sem=win_send.at[row], recv_sem=win_recv.at[row], device_id=(j, me_r), device_id_type=MESH)
+
+    def return_copy(clipped, target, row, d):
         return pltpu.make_async_remote_copy(
             src_ref=clipped.at[pl.ds(FL * d, FL)], dst_ref=target(me_f),
-            send_sem=ret_send.at[which, d], recv_sem=ret_recv.at[which, me_f],
-            device_id=(d, me_r), device_id_type=MESH)
-
-    def return_wait(target, which, j):
-        pltpu.make_async_remote_copy(
-            src_ref=target(j), dst_ref=target(j), send_sem=ret_send.at[which, 0],
-            recv_sem=ret_recv.at[which, j], device_id=(j, me_r), device_id_type=MESH).wait_recv()
+            send_sem=ret_send.at[row], recv_sem=ret_recv.at[row], device_id=(d, me_r), device_id_type=MESH)
+
+    def wait_tiles(buffer, count, sem):
+        tiles = buffer.at[pl.ds(0, count)]
+        pltpu.make_async_copy(tiles, tiles, sem).wait()
 
     def window(landing, clipped, starts):
         half = lax.broadcasted_iota(jnp.int32, (NF * FL, 128), 1) < 64
@@ -386,6 +390,16 @@
 
     def window_tasks(which, tag, members, source, sends, landing, clipped, starts, target, rank):
         inside = (me_f >= members[0]) & (me_f <= members[-1])
+        returns = sends[0][1]
+
+        def others(run):
+            @pl.when(inside)
+            def _():
+                run(len(members) - 1)
+
+            @pl.when(jnp.logical_not(inside))
+            def _():
+                run(len(members))
 
         def scatter(freqs, row):
             def run():
@@ -404,48 +418,35 @@
         def apply():
             @pl.when(inside)
             def _():
-                for sender in range(NF):
-                    @pl.when(me_f != sender)
-                    def _():
-                        for freqs, row, _deps in sends:
-                            in_wait(landing, freqs, row, sender)
-
+                for freqs, row, _deps in sends:
+                    wait_tiles(landing, (NF - 1) * freqs[1], win_recv.at[row])
                 window(landing, clipped, starts)
                 for d in range(NF):
                     @pl.when(me_f != d)
                     def _():
-                        return_copy(clipped, target, which, d).start()
+                        return_copy(clipped, target, returns, d).start()
 
                 target(me_f)[...] = clipped[pl.ds(FL * me_f, FL)]
 
+        def drain():
+            for freqs, row, _deps in sends:
+                others(lambda n: wait_tiles(landing, n * freqs[1], win_send.at[row]))
+
+            @pl.when(inside)
+            def _():
+                wait_tiles(landing, (NF - 1) * FL, ret_send.at[returns])
+
         def collect():
+            others(lambda n: wait_tiles(landing, n * FL, ret_recv.at[returns]))
             if which == 1:
                 drain()
-            for j in members:
-                @pl.when(me_f != j)
-                def _():
-                    return_wait(target, which, j)
-
-        def drain():
-            for j in members:
-                @pl.when(me_f != j)
-                def _():
-                    for freqs, row, _deps in sends:
-                        out_copy(source, freqs, landing, row, j).wait_send()
-
-            @pl.when(inside)
-            def _():
-                for d in range(NF):
-                    @pl.when(me_f != d)
-                    def _():
-                        return_copy(clipped, target, which, d).wait_send()
 
         if which == 0:
             plan.add(tag + "drain", (tag + "in",) + ("w1in",), drain, dur=0.3, rank=(5,))
         outs = []
         for freqs, row, deps in sends:
             outs.append(f"{tag}out{row}")
-            plan.add(outs[-1], deps, scatter(freqs, row), ("x", 0), len(members) * 8 * freqs[1] * 340, 0.2, rank)
+            plan.add(outs[-1], deps, scatter(freqs, row), ("x", 0), len(members) * 8 * freqs[1] * 340, 0.2, rank if which == 0 else (2, 9))
         plan.add(tag + "win", outs, apply, ("x", 1), len(members) * 8 * FL * 340, 1.5, rank)
         plan.add(tag + "in", (tag + "win",), collect, dur=0.2, rank=rank)
 
@@ -460,7 +461,7 @@
 
         members = tuple(range(MEMBERS * h, MEMBERS * h + MEMBERS))
         window_tasks(0, f"w{h}", members, functools.partial(block_of, part, h),
-                     [((0, FL), 0, (f"own{h}", "onset"))], x1, y1, onset_summed,
+                     [((0, FL), h, (f"own{h}", "onset"))], x1, y1, onset_summed,
                      functools.partial(block_of, gathered, h), (0, h, 0))
 
     def gather_piece(name, freqs, dz, dy, h, target, deps, link, rank):
@@ -488,15 +489,15 @@
         own = f"w{h}in"
         deep = NZ // 2
         for sign in (1, -1):
-            gather_piece(f"ya{h},{sign},0", PARTS["a"], 0, 0, h, rec_of(0, sign), (own,), ("y", sign), (2, h, 0))
-            gather_piece(f"zb{h},{sign},0", PARTS["b"], 0, 0, h, rec_of(sign, 0), (own,), ("z", sign), (2, h, 0))
+            gather_piece(f"ya{h},{sign},0", PARTS["a"], 0, 0, h, rec_of(0, sign), (own,), ("y", sign), (2, 0, h))
+            gather_piece(f"zb{h},{sign},0", PARTS["b"], 0, 0, h, rec_of(sign, 0), (own,), ("z", sign), (2, 0, h))
         for sign in (1, -1):
             gather_piece(f"ya{h},{sign},1", halves("a", sign), 0, -sign, h, rec_of(0, sign), (f"ya{h},{sign},0",),
-                         ("y", sign), (2, h, 0))
+                         ("y", sign), (2, 0, h))
             for k in range(1, deep):
                 freqs = halves("b", sign) if k == deep - 1 else PARTS["b"]
                 gather_piece(f"zb{h},{sign},{k}", freqs, -sign * k, 0, h, rec_of(sign, 0), (f"zb{h},{sign},{k - 1}",),
-                             ("z", sign), (2, h, 0))
+                             ("z", sign), (2, 0, h))
         for dy in (0, -1, 1, 2):
             if dy == 0:
                 deps = (own,)
@@ -509,7 +510,7 @@
                     if k == deep - 1 and dy not in both_y[sign]:
                         continue
                     gather_piece(f"za{h},{sign},{k},{dy}", PARTS["a"], -sign * k, dy, h, rec_of(sign, 0),
-                                 deps if k == 0 else (f"za{h},{sign},{k - 1},{dy}",), ("z", sign), (2, h, 1, k))
+                                 deps if k == 0 else (f"za{h},{sign},{k - 1},{dy}",), ("z", sign), (2, 1, h, k))
                     ends[h, "a"].append(f"za{h},{sign},{k},{dy}")
         for dz in (0, -1, 1, -2, 2, -3, 3, 4):
             if dz == 0:
@@ -524,7 +525,7 @@
                     if k == 1 and dz not in both_z[sign]:
                         continue
                     gather_piece(f"yb{h},{sign},{k},{dz}", PARTS["b"], dz, -sign * k, h, rec_of(0, sign),
-                                 deps if k == 0 else (f"yb{h},{sign},0,{dz}",), ("y", sign), (2, h, 1, k))
+                                 deps if k == 0 else (f"yb{h},{sign},0,{dz}",), ("y", sign), (2, 1, h, k))
                     ends[h, "b"].append(f"yb{h},{sign},{k},{dz}")
         for name in list(copies):
             if name.startswith((f"ya{h}", f"zb{h}")):
@@ -550,8 +551,7 @@
                     made[f] = total[:ROWS] + jnp.where(low_half, -turned, turned)
                 return _
 
-            for f in freqs:
-                step(f, 0)
+            each(freqs, step, FWD)
 
         return run
 
@@ -567,7 +567,7 @@
                          dur=3.4 / CHUNKS * len(freqs) / FL, rank=(3, h))
 
     window_tasks(1, "v", tuple(range(ROWS // 8)), lambda j: made.at[:, pl.ds(8 * j, 8), :],
-                 [(PARTS[name], 1 + place, last[name]) for place, name in enumerate(("b", "a"))], x2, y2, onset_here,
+                 [(PARTS[name], CHUNKS + place, last[name]) for place, name in enumerate(("b", "a"))], x2, y2, onset_here,
                  lambda j: back.at[:, pl.ds(8 * j, 8), :], (4,))
 
     order = plan.order()
@@ -581,12 +581,12 @@
     for phase, buffer in enumerate((part, gathered)):
         amount = buffer.reshape(CHUNKS * FL * NZ * NY, NR, 128).at[pl.ds(0, blocks)]
         pltpu.make_async_copy(amount, amount, send_sem.at[phase]).wait()
-    out[...] = back[...]
+    out[...] = initial[...] - back[...]
     kernel.plan = plan
     kernel.ordered = order
 
 
-def iterate(response_real, response_imaginary, focus, onset, inv, fwd):
+def iterate(response_real, response_imaginary, focus, onset, inv, fwd, initial):
     na, nb = SPLIT, FL - SPLIT
     vmem = pl.BlockSpec(memory_space=pltpu.VMEM)
     scratch = [
@@ -594,7 +594,8 @@
         pltpu.VMEM(onset.shape, jnp.int32),
         pltpu.VMEM(inv.shape, BF),
         pltpu.VMEM(fwd.shape, BF),
-        pltpu.SemaphoreType.DMA((4,)),
+        pltpu.VMEM(focus.shape, F32),
+        pltpu.SemaphoreType.DMA((5,)),
         pltpu.VMEM((FL, 2 * ROWS, response_real.shape[2]), F32),
         pltpu.SemaphoreType.DMA((2, CHUNKS, 2)),
         pltpu.VMEM((FL, CHUNKS, NZ, NY, NR, 128), F32),
@@ -616,28 +617,29 @@
         pltpu.SemaphoreType.DMA((CHUNKS,)),
         pltpu.SemaphoreType.DMA((2,)),
         pltpu.SemaphoreType.DMA((2 * CHUNKS - 1, 64)),
-        pltpu.SemaphoreType.DMA((3, NF)),
-        pltpu.SemaphoreType.DMA((3, NF)),
-        pltpu.SemaphoreType.DMA((2, NF)),
-        pltpu.SemaphoreType.DMA((2, NF)),
+        pltpu.SemaphoreType.DMA((CHUNKS + 2,)),
+        pltpu.SemaphoreType.DMA((CHUNKS + 2,)),
+        pltpu.SemaphoreType.DMA((CHUNKS + 1,)),
+        pltpu.SemaphoreType.DMA((CHUNKS + 1,)),
     ]
     return pl.pallas_call(
         kernel,
         out_shape=jax.ShapeDtypeStruct((FL, ROWS, 128), F32),
-        in_specs=[pl.BlockSpec(memory_space=pl.ANY)] * 6,
+        in_specs=[pl.BlockSpec(memory_space=pl.ANY)] * 7,
         out_specs=vmem,
         scratch_shapes=scratch,
         compiler_params=pltpu.CompilerParams(
             collective_id=0, has_side_effects=True, vmem_limit_bytes=60 * 1024 * 1024
         ),
-    )(response_real, response_imaginary, focus, onset, inv, fwd)
+    )(response_real, response_imaginary, focus, onset, inv, fwd, initial)
 
 
 def on_device(response_real, response_imaginary, focus, initial, onset):
     inv, fwd = dft_tables(NF * FL)
     by_freq = jnp.transpose(focus, (1, 0, 2))
-    update = iterate(response_real, response_imaginary, by_freq, onset, jnp.asarray(inv), jnp.asarray(fwd))
-    return initial - jnp.transpose(update, (1, 0, 2))
+    update = iterate(response_real, response_imaginary, by_freq, onset, jnp.asarray(inv), jnp.asarray(fwd),
+                     jnp.transpose(initial, (1, 0, 2)))
+    return jnp.transpose(update, (1, 0, 2))
 
 
 def solution(mesh):

time: 136 us -> 131 us (0.963)
  Pallas kernels: 134 us -> 129 us
  other arithmetic: 1.71 us -> 0 us
  local copies, waits for them, and re-layouts: 0.01 us -> 1.69 us
    pallas_call x1, Pallas kernels: 134 us -> 129 us  [iterate(): pl.pallas_call(kernel, out_shape=jax.ShapeDtypeStruct((FL, ROWS, 128), F3...]
    sub x1 -> x0, other arithmetic: 1.71 us -> none  [on_device(): return initial - jnp.transpose(update, (1, 0, 2))]
    unnamed x2 -> x1, local copies, waits for them, and re-layouts: 0.01 us -> 1.69 us
where the time goes in v4:
time: 131 us; the launch traced here: 130 us
  Pallas kernels  129 us (98%)
  local copies, waits for them, and re-layouts  1.69 us (1%)
    pallas_call x1, Pallas kernels, iterate(): pl.pallas_call(kernel, out_shape=jax.ShapeDtypeStruct((FL, ROWS, 128), F3...  129 us

profile of v4, /device:TPU:1, one launch (start us, length us, event | category | flops | bytes accessed | tf_op | source)
XLA Modules:
  0.0 130.4 jit_solution(3106220566635522847)
XLA Ops:
  0.0 128.7 %shard_map.73 = f32[12,48,128]{2,1,0:T(8,128)} custom-call(f32[12,48,1536]{2,1,0:T(8,128)} %rr.1, f32[12,48,1536]{2,1,0:T(8,128)} %ri.1, f32[12,48,128]{2,1,0:T(8,128)} %bitcast.4, s32[48,64]{1,0:T(8,128)} %onset_in.1, bf16[192,576]{1,0:T(8,128)(2,1)} %constant.4.clone.inv_in, bf16[192,576]{1,0:T(8,128)(2,1)} %constant.5.clone.fwd_in, f32[12,48,128]{2,1,0:T(8,128)} %bitcast.5), custom_call_target="tpu_custom_call" | custom-call | tf_op jit(solution)/shard_map/pallas_call | solution.py:625
  128.7 1.7 %copy.9 = f32[48,12,128]{2,0,1:T(8,128)} copy(f32[48,12,128]{2,0,1:T(8,128)} %bitcast.3) | data formatting | bytes 589824

commit v5 on v4

--- a/solution.py
+++ b/solution.py
@@ -26,7 +26,7 @@
 LATENCY = 1.8
 ADJ, FWD = 0, 0
 X_LATENCY = 4.0
-BACKLOG = 1.0
+BACKLOG = 1.4
 
 
 def split(value):
@@ -198,15 +198,25 @@
     plan = Plan()
     copies = {}
 
-    used = {}
-
-    def piece(name, src, dst, target, phase, h):
-        bank = h if phase == 0 else (CHUNKS + h if h < CHUNKS - 1 else 0)
-        index = used[phase, h] = used.get((phase, h), -1) + 1
+    used, groups_of, units = {}, {}, {}
+
+    def piece(name, src, dst, target, phase, h, size, group):
+        bank = h if phase == 0 else (CHUNKS if h == 0 else h - 1)
+        key = (phase, h, group or name)
+        if key not in groups_of:
+            used[phase, h] = used.get((phase, h), -1) + 1
+            groups_of[key] = recv_sem.at[bank, used[phase, h]]
+            units[key] = 0
+        units[key] += size
         copies[name] = pltpu.make_async_remote_copy(
-            src_ref=src, dst_ref=dst, send_sem=send_sem.at[phase], recv_sem=recv_sem.at[bank, index],
+            src_ref=src, dst_ref=dst, send_sem=send_sem.at[phase], recv_sem=groups_of[key],
             device_id=(me_f, target), device_id_type=MESH)
         return copies[name]
+
+    def wait_group(phase, h, group):
+        key = (phase, h, group)
+        amount = part.reshape(CHUNKS * FL * NZ * NY, NR, 128).at[pl.ds(0, units[key])]
+        pltpu.make_async_copy(amount, amount, groups_of[key]).wait()
 
     def each(freqs, step, together):
         whole = len(freqs) // together * together if together else 0
@@ -273,11 +283,11 @@
         slot[kind] += 1
         return stages[kind].at[index, pl.ds(0, count)]
 
-    def reduce_piece(name, kind, freqs, dz, dy, h, target, adds, deps, link, rank):
+    def reduce_piece(name, kind, freqs, dz, dy, h, target, adds, deps, link, rank, group=None):
         start, count = freqs
         src = part.at[pl.ds(start, count), h, at_z(dz), at_y(dy)]
         dst = staging(kind, count)
-        copy = piece(name, src, dst, target, 0, h)
+        copy = piece(name, src, dst, target, 0, h, count, group)
         copies[name] = (copy, dst, start, count)
 
         def run():
@@ -286,10 +296,13 @@
 
         plan.add(name, tuple(adds) + tuple(deps), run, link, count * NR * 512, 0.12, rank)
 
-    def take(adds, dz, dy, h):
+    def take(adds, dz, dy, h, group=None):
+        if group:
+            wait_group(0, h, group)
         for other in adds:
             copy, dst, start, count = copies[other]
-            copy.wait_recv()
+            if not group:
+                copy.wait_recv()
             where = (pl.ds(start, count), h, at_z(dz), at_y(dy))
             part[where] += dst[...]
 
@@ -306,7 +319,7 @@
                         continue
                     adds = [f"a1{h},{sign},{k + 1},{dy}"] if (k < deep - 1 or (k == deep - 1 and dy in both_y[sign])) else []
                     reduce_piece(f"a1{h},{sign},{k},{dy}", "a1", PARTS["a"], sign * k, dy, h, rec_of(sign, 0), adds,
-                                 adjoint_done[h, "a"], ("z", sign), (1, h, 0, -k, place))
+                                 adjoint_done[h, "a"], ("z", sign), (1, h, 0, -k, place), f"a1{dy}" if k == 1 else None)
         for k in (2, 1):
             for place, dz in enumerate(order_z):
                 for sign in (1, -1):
@@ -314,14 +327,14 @@
                         continue
                     adds = [f"b1{h},{sign},2,{dz}"] if k == 1 and dz in both_z[sign] else []
                     reduce_piece(f"b1{h},{sign},{k},{dz}", "b1", PARTS["b"], dz, sign * k, h, rec_of(0, sign), adds,
-                                 adjoint_done[h, "b"], ("y", sign), (1, h, 0, -k, place))
+                                 adjoint_done[h, "b"], ("y", sign), (1, h, 0, -k, place), f"b1{dz}" if k == 1 else None)
 
         def first_sum(name, kind, d):
             keys = [f"{kind}{h},{sign},1,{d}" for sign in (1, -1)]
 
             def run(keys=keys, d=d, h=h, kind=kind):
                 dz, dy = (0, d) if kind == "a1" else (d, 0)
-                take(keys, dz, dy, h)
+                take(keys, dz, dy, h, f"{kind}{d}")
 
             plan.add(name, keys, run, dur=0.12, rank=(0, h, 0))
 
@@ -333,18 +346,18 @@
             reduce_piece(f"a2{h},{sign},2", "a2", halves("a", sign), 0, 2 * sign, h, rec_of(0, sign), [],
                          (f"as{h},2",), ("y", sign), (0, h, 1, -2))
             reduce_piece(f"a2{h},{sign},1", "a2", PARTS["a"], 0, sign, h, rec_of(0, sign), [f"a2{h},{sign},2"],
-                         (f"as{h},{sign}",), ("y", sign), (0, h, 1, -1))
+                         (f"as{h},{sign}",), ("y", sign), (0, h, 1, -1), "own")
             for k in range(deep, 0, -1):
                 freqs = halves("b", sign) if k == deep else PARTS["b"]
                 adds = [] if k == deep else [f"b2{h},{sign},{k + 1}"]
                 source = 4 if k == deep else sign * k
                 reduce_piece(f"b2{h},{sign},{k}", "b2", freqs, sign * k, 0, h, rec_of(sign, 0), adds,
-                             (f"bs{h},{source}",), ("z", sign), (0, h, 1, -k))
+                             (f"bs{h},{source}",), ("z", sign), (0, h, 1, -k), "own" if k == 1 else None)
 
         own_keys = [f"a2{h},{sign},1" for sign in (1, -1)] + [f"b2{h},{sign},1" for sign in (1, -1)]
 
         def own_sum(keys=tuple(own_keys), h=h):
-            take(keys, 0, 0, h)
+            take(keys, 0, 0, h, "own")
 
         plan.add(f"own{h}", own_keys + [f"as{h},0", f"bs{h},0"], own_sum, dur=0.2, rank=(0, h, 0))
 
@@ -464,10 +477,14 @@
                      [((0, FL), h, (f"own{h}", "onset"))], x1, y1, onset_summed,
                      functools.partial(block_of, gathered, h), (0, h, 0))
 
-    def gather_piece(name, freqs, dz, dy, h, target, deps, link, rank):
+    received, together = set(), set()
+
+    def gather_piece(name, freqs, dz, dy, h, target, deps, link, rank, group=None):
         start, count = freqs
         where = gathered.at[pl.ds(start, count), h, at_z(dz), at_y(dy)]
-        copy = piece(name, where, where, target, 1, h)
+        copy = piece(name, where, where, target, 1, h, count, group)
+        if group:
+            together.add(name)
         arrivals = [dep for dep in deps if dep in copies]
 
         def run():
@@ -477,10 +494,9 @@
 
         plan.add(name, deps, run, link, count * NR * 512, 0.08, rank)
 
-    received = set()
 
     def receive(name):
-        if name not in received:
+        if name not in received and name not in together:
             received.add(name)
             copies[name].wait_recv()
 
@@ -510,7 +526,8 @@
                     if k == deep - 1 and dy not in both_y[sign]:
                         continue
                     gather_piece(f"za{h},{sign},{k},{dy}", PARTS["a"], -sign * k, dy, h, rec_of(sign, 0),
-                                 deps if k == 0 else (f"za{h},{sign},{k - 1},{dy}",), ("z", sign), (2, 1, h, k))
+                                 deps if k == 0 else (f"za{h},{sign},{k - 1},{dy}",), ("z", sign), (2, 1, h, k),
+                                 None if k < deep - 2 or (k == deep - 2 and dy in both_y[sign]) else "a")
                     ends[h, "a"].append(f"za{h},{sign},{k},{dy}")
         for dz in (0, -1, 1, -2, 2, -3, 3, 4):
             if dz == 0:
@@ -525,7 +542,8 @@
                     if k == 1 and dz not in both_z[sign]:
                         continue
                     gather_piece(f"yb{h},{sign},{k},{dz}", PARTS["b"], dz, -sign * k, h, rec_of(0, sign),
-                                 deps if k == 0 else (f"yb{h},{sign},0,{dz}",), ("y", sign), (2, 1, h, k))
+                                 deps if k == 0 else (f"yb{h},{sign},0,{dz}",), ("y", sign), (2, 1, h, k),
+                                 None if k == 0 and dz in both_z[sign] else "b")
                     ends[h, "b"].append(f"yb{h},{sign},{k},{dz}")
         for name in list(copies):
             if name.startswith((f"ya{h}", f"zb{h}")):
@@ -533,8 +551,10 @@
 
     def forward(freqs, h, name):
         def run():
-            for key in ends[h, name]:
-                receive(key)
+            if freqs[0] == PARTS[name][0]:
+                for key in ends[h, name]:
+                    receive(key)
+                wait_group(1, h, name)
 
             def step(f, _):
                 high, low = split(resp[f, :, pl.ds(COLS * h, COLS)])
@@ -582,7 +602,7 @@
         amount = buffer.reshape(CHUNKS * FL * NZ * NY, NR, 128).at[pl.ds(0, blocks)]
         pltpu.make_async_copy(amount, amount, send_sem.at[phase]).wait()
     out[...] = initial[...] - back[...]
-    kernel.plan = plan
+    kernel.plan, kernel.used = plan, used
     kernel.ordered = order
 
 
@@ -616,7 +636,7 @@
         pltpu.SemaphoreType.DMA((CHUNKS,)),
         pltpu.SemaphoreType.DMA((CHUNKS,)),
         pltpu.SemaphoreType.DMA((2,)),
-        pltpu.SemaphoreType.DMA((2 * CHUNKS - 1, 64)),
+        pltpu.SemaphoreType.DMA((CHUNKS + 1, 49)),
         pltpu.SemaphoreType.DMA((CHUNKS + 2,)),
         pltpu.SemaphoreType.DMA((CHUNKS + 2,)),
         pltpu.SemaphoreType.DMA((CHUNKS + 1,)),

time: 131 us -> 130 us (level)
  no operation moved by 1% of the time
where the time goes in v5:
time: 130 us; the launch traced here: 129 us
  Pallas kernels  128 us (98%)
  local copies, waits for them, and re-layouts  1.69 us (1%)
    pallas_call x1, Pallas kernels, iterate(): pl.pallas_call(kernel, out_shape=jax.ShapeDtypeStruct((FL, ROWS, 128), F3...  128 us

profile of v5, /device:TPU:1, one launch (start us, length us, event | category | flops | bytes accessed | tf_op | source)
XLA Modules:
  0.0 129.4 jit_solution(8211905436003790354)
XLA Ops:
  0.0 127.7 %shard_map.73 = f32[12,48,128]{2,1,0:T(8,128)} custom-call(f32[12,48,1536]{2,1,0:T(8,128)} %rr.1, f32[12,48,1536]{2,1,0:T(8,128)} %ri.1, f32[12,48,128]{2,1,0:T(8,128)} %bitcast.4, s32[48,64]{1,0:T(8,128)} %onset_in.1, bf16[192,576]{1,0:T(8,128)(2,1)} %constant.4.clone.inv_in, bf16[192,576]{1,0:T(8,128)(2,1)} %constant.5.clone.fwd_in, f32[12,48,128]{2,1,0:T(8,128)} %bitcast.5), custom_call_target="tpu_custom_call" | custom-call | tf_op jit(solution)/shard_map/pallas_call | solution.py:645
  127.7 1.7 %copy.9 = f32[48,12,128]{2,0,1:T(8,128)} copy(f32[48,12,128]{2,0,1:T(8,128)} %bitcast.3) | data formatting | bytes 589824
